TPU v7x, 256 devices: a whole 4x4x8 slice. The times are simulated.
256 devices in a mesh: gx: 8 (over x, core), gy: 4 (over z_hi), gz: 8 (over z_lo, y).
Axes of the slice: x: 4, y: 4, z: 8 (z_hi: 4, z_lo: 2; z = z_hi * 2 + z_lo), core: 2. Of those that a mesh axis runs over, the one named last changes fastest.
Arguments:
- hidden_rows: bfloat16 [4096, 16384], P(('gx', 'gy'), 'gz'), may hold values from -2000 to 2000
- norm_gain: bfloat16 [16384], P('gz'), may hold values from 0.5 to 1.5
- w_query: bfloat16 [16384, 16384], P('gz', ('gx', 'gy')), may hold values from -0.046875 to 0.046875
- w_keyval: bfloat16 [16384, 2048], P('gz', ('gx', 'gy')), may hold values from -0.046875 to 0.046875
- positions: int32 [4096], P('gz'), may hold values from 0 to 1023, as said below
- keyval_order: int32 [8], replicated, may hold values from 0 to 7, each once
Outputs:
- queries: bfloat16 [4096, 16384], P('gz', ('gx', 'gy'))
- keyval_owned: bfloat16 [8, 4096, 256], P('gy', 'gz')
Inputs may be any that keep to these rules, and one draw needn't show every extreme that they name: `positions`: each token's position within its packed document: 0 where a document starts, else one more than the previous token's; a document holds at most 1024 tokens. `keyval_order`: each head once.
All inputs are finite; a program needn't handle non-finite values.
Results may differ from a plain program's by a relative error of at most 0.0066.
Values may be sent and summed in bfloat16 or wider, within the bound.
No kernel may reach another device: no remote copies, remote signals or barrier semaphores. Data moves between devices by JAX's collectives and lax.ppermute only.
A program may use at most 128 MiB of HBM per device.

v0:
```python
import math

import jax
import jax.numpy as jnp
from jax import lax
from jax.sharding import PartitionSpec as P

D = 16384
KVH = 8
HD = 128


rope_base = 500000.0
norm_eps = 1e-05


def from_everyone(value, axis):
    copies = jnp.broadcast_to(value, (lax.axis_size(axis), *value.shape))
    return lax.all_to_all(copies, axis, split_axis=0, concat_axis=0, tiled=True)


def taken_together(value, axis):
    everything = from_everyone(value, axis)
    return jnp.sum(everything, axis=0)


def in_blocks(value, dim, count):
    before, after = (value.shape[:dim], value.shape[dim + 1 :])
    return jnp.moveaxis(value.reshape(*before, count, -1, *after), dim, 0)


def summed_on_arrival(value, axis, dim):
    count = lax.axis_size(axis)
    blocks = lax.all_to_all(in_blocks(value, dim, count), axis, 0, 0, tiled=True)
    return jnp.sum(blocks.astype(jnp.float32), axis=0)


def rotate_pairs(values, position_ids, col_start, keys_only):
    row_total, col_width = values.shape
    pair_col = col_start + 2 * jnp.arange(col_width // 2, dtype=jnp.int32)
    within = pair_col % HD
    inv_freq = jnp.exp((within // 2).astype(jnp.float32) * (-2.0 * math.log(rope_base) / HD))
    angles = position_ids.astype(jnp.float32)[:, None] * inv_freq[None, :]
    cosines = jnp.cos(angles)
    sine_part = jnp.sin(angles)
    paired = values.reshape(row_total, col_width // 2, 2)
    even_part = paired[..., 0]
    odd_part = paired[..., 1]
    rotated = jnp.stack(
        [even_part * cosines - odd_part * sine_part, even_part * sine_part + odd_part * cosines],
        axis=-1,
    )
    if keys_only:
        is_key = (pair_col // HD % 2 == 0)[None, :, None]
        rotated = jnp.where(is_key, rotated, paired)
    return rotated.reshape(row_total, col_width)


def body(hidden_rows, norm_gain, w_query, w_keyval, positions, keyval_order):
    widened_gain = norm_gain.astype(jnp.float32)
    widened = hidden_rows.astype(jnp.float32)
    factor = lax.rsqrt(taken_together(jnp.sum(widened * widened, axis=1), "gz") / D + norm_eps)
    normed_rows = (
        hidden_rows.astype(jnp.float32) * factor[:, None] * widened_gain[None, :]
    ).astype(jnp.bfloat16)
    query_width = w_query.shape[1]
    keyval_width = w_keyval.shape[1]
    group_size = lax.axis_size("gy")
    gathered = lax.all_gather(normed_rows, ("gx", "gy"), axis=0, tiled=True)
    query_sum = summed_on_arrival(
        jnp.dot(gathered, w_query, preferred_element_type=jnp.float32).astype(jnp.bfloat16), "gz", 0
    )
    keyval_sum = summed_on_arrival(
        jnp.dot(gathered, w_keyval, preferred_element_type=jnp.float32).astype(jnp.bfloat16),
        "gz",
        0,
    )
    col_index = lax.axis_index("gx") * group_size + lax.axis_index("gy")
    queries = rotate_pairs(query_sum, positions, col_index * query_width, False).astype(
        jnp.bfloat16
    )
    keyval_part = rotate_pairs(keyval_sum, positions, col_index * keyval_width, True).astype(
        jnp.bfloat16
    )
    keyval_all = lax.all_gather(keyval_part, ("gx", "gy"), axis=1, tiled=True)
    slot_count = KVH // group_size
    first_slot = lax.axis_index("gy") * slot_count
    keyval_heads = keyval_all.reshape(keyval_all.shape[0], KVH, 2 * HD)
    wanted = lax.dynamic_slice_in_dim(keyval_order, first_slot, slot_count, 0)
    selector = (wanted[:, None] == jnp.arange(KVH, dtype=jnp.int32)[None, :]).astype(jnp.bfloat16)
    keyval_owned = jnp.einsum(
        "sh,rhc->src", selector, keyval_heads, preferred_element_type=jnp.float32
    ).astype(jnp.bfloat16)
    return (queries, keyval_owned)


def solution(mesh):
    in_specs = (
        P(("gx", "gy"), "gz"),
        P("gz"),
        P("gz", ("gx", "gy")),
        P("gz", ("gx", "gy")),
        P("gz"),
        P(),
    )
    out_specs = (P("gz", ("gx", "gy")), P("gy", "gz", None))
    return jax.shard_map(body, mesh=mesh, in_specs=in_specs, out_specs=out_specs, check_vma=False)
```

profile of v0, /device:TPU:1, one launch (start us, length us, event | category | flops | bytes accessed | tf_op | source)
XLA Modules:
  0.0 268.1 jit_solution(16777390107375378753)
XLA Ops:
  7.2 0.0 copy-start
  7.2 1.4 fusion
  8.6 0.6 broadcast_in_dim.14
  9.2 6.4 %all-to-all-start = ((f32[8,1,128]{2,1,0:T(1,128)}), f32[8,1,128]{2,1,0:T(1,128)S(1)}, u32[]{:S(2)}, u32[]{:S(2)}) async-start(f32[8,1,128]{2,1,0:T(1,128)} %broadcast_in_dim.14), calls=%async_computation | async-start | bytes 8192 | tf_op jit(solution)/shard_map/all_to_all | solution.py:19
  15.5 0.0 all-gather.3.cloned.1.call-start
  15.6 0.7 convert_element_type.52
  16.3 4.2 %all-to-all-done = f32[8,1,128]{2,1,0:T(1,128)S(1)} async-done(((f32[8,1,128]{2,1,0:T(1,128)}), f32[8,1,128]{2,1,0:T(1,128)S(1)}, u32[]{:S(2)}, u32[]{:S(2)}) %all-to-all-start) | async-done | bytes 4128 | tf_op jit(solution)/shard_map/all_to_all | solution.py:19
  20.5 2.0 fusion.2
  22.5 0.0 all-gather.3.cloned.1.call-update
  22.6 107.4 %all-gather.3.cloned.1.call-done = bf16[4096,2048]{1,0:T(8,128)(2,1)} async-done(((bf16[128,2048]{1,0:T(8,128)(2,1)}), bf16[4096,2048]{1,0:T(8,128)(2,1)}) %all-gather.3.cloned.1.call-update) | async-done | bytes 16777232 | tf_op jit(solution)/shard_map/all_gather | solution.py:69
  130.0 10.9 %convolution_convert_fusion.1 = bf16[4096,64]{0,1:T(8,128)(2,1)S(1)} fusion(bf16[4096,2048]{1,0:T(8,128)(2,1)} %all-gather.3.cloned.1.call-done, bf16[2048,64]{0,1:T(8,128)(2,1)} %param.9), kind=kOutput, calls=%fused_computation.2 | convolution fusion | flops 1074003968 | bytes 17563648 | tf_op jit(solution)/shard_map/dot_general | solution.py:74
  140.9 0.8 copy.51
  141.8 18.8 %all-to-all-start.2 = ((bf16[8,512,64]{1,2,0:T(8,128)(2,1)}), bf16[8,512,64]{1,2,0:T(8,128)(2,1)S(1)}, u32[]{:S(2)}, u32[]{:S(2)}) async-start(bf16[8,512,64]{1,2,0:T(8,128)(2,1)} %bitcast.22), calls=%async_computation.2 | async-start | bytes 1048576 | tf_op jit(solution)/shard_map/all_to_all | solution.py:34
  160.6 0.0 copy-done
  160.6 13.7 %convolution_convert_fusion = bf16[4096,512]{1,0:T(8,128)(2,1)} fusion(bf16[4096,2048]{1,0:T(8,128)(2,1)} %all-gather.3.cloned.1.call-done, bf16[2048,512]{1,0:T(8,128)(2,1)S(1)} %copy-done), kind=kOutput, calls=%fused_computation.1 | convolution fusion | flops 8592031744 | bytes 23068672 | tf_op jit(solution)/shard_map/dot_general | solution.py:71
  174.4 0.0 all-to-all-done.2
  174.4 0.0 copy-start.1
  174.4 0.0 copy-start.2
  174.4 5.3 %all-to-all-start.1 = ((bf16[8,512,512]{2,1,0:T(8,128)(2,1)}), bf16[8,512,512]{2,1,0:T(8,128)(2,1)}, u32[]{:S(2)}, u32[]{:S(2)}) async-start(bf16[8,512,512]{2,1,0:T(8,128)(2,1)} %bitcast.23), calls=%async_computation.1 | async-start | bytes 8388608 | tf_op jit(solution)/shard_map/all_to_all | solution.py:34
  179.6 0.2 all-gather.5.cloned.1.call-start
  179.9 0.0 copy-done.1
  179.9 0.1 broadcast_in_dim.15
  180.0 0.1 broadcast_in_dim.26
  180.1 0.1 convert_reduce_fusion.1
  180.2 0.1 reshape.314
  180.3 0.1 fusion.25
  180.4 0.3 fusion.15
  180.8 0.1 copy.36
  180.9 0.7 select_convert_fusion
  181.6 0.0 all-gather.5.cloned.1.call-update
  181.6 0.0 copy-done.2
  181.6 0.1 dynamic_slice.3
  181.7 57.3 %all-gather.5.cloned.1.call-done = bf16[512,2048]{0,1:T(8,128)(2,1)} async-done(((bf16[512,64]{0,1:T(8,128)(2,1)}), bf16[512,2048]{0,1:T(8,128)(2,1)}) %all-gather.5.cloned.1.call-update) | async-done | bytes 2097168 | tf_op jit(solution)/shard_map/all_gather | solution.py:85
  239.0 4.6 %copy.40 = bf16[512,8,256]{2,1,0:T(8,128)(2,1)} copy(bf16[512,8,256]{0,2,1:T(8,128)(2,1)} %bitcast.25) | data formatting | bytes 4194304 | tf_op jit(solution)/shard_map/reshape | solution.py:88
  243.6 2.3 convolution_convert_fusion.2
  245.9 0.9 copy.39
  246.8 0.0 all-to-all-done.1
  246.8 2.9 %convert_reduce_fusion = f32[512,512]{1,0:T(8,128)S(1)} fusion(bf16[8,512,512]{2,1,0:T(8,128)(2,1)} %all-to-all-done.1), kind=kLoop, calls=%fused_computation | loop fusion | flops 3932160 | bytes 5242880 | tf_op jit(solution)/shard_map/reduce_sum | solution.py:35
  249.7 1.3 copy.29
  251.0 1.8 reshape.312
  252.8 1.8 fusion.24
  254.6 1.2 copy.41
  255.9 1.2 copy.42
  257.1 2.4 fusion.8
  259.5 0.1 pad_maximum_fusion
  259.5 0.5 copy.32
  260.1 0.2 convert_element_type.58
  260.3 1.0 copy.38
  (8 shorter events, 0.1 us)
Async XLA Ops:
  7.2 153.5 %copy-start = (bf16[2048,512]{1,0:T(8,128)(2,1)S(1)}, bf16[2048,512]{1,0:T(8,128)(2,1)}, u32[]{:S(2)}) copy-start(bf16[2048,512]{1,0:T(8,128)(2,1)} %param.8) | copy-start | bytes 6291460
  9.2 11.3 %all-to-all-start = ((f32[8,1,128]{2,1,0:T(1,128)}), f32[8,1,128]{2,1,0:T(1,128)S(1)}, u32[]{:S(2)}, u32[]{:S(2)}) async-start(f32[8,1,128]{2,1,0:T(1,128)} %broadcast_in_dim.14), calls=%async_computation | async-start | bytes 8192 | tf_op jit(solution)/shard_map/all_to_all | solution.py:19
  15.5 114.5 %all-gather.3.cloned.1.call-start = ((), (), s32[]{:S(2)}) async-start(), calls=%async_computation.3 | async-start | bytes 17301504 | tf_op jit(solution)/shard_map/all_gather | solution.py:69
  141.8 32.6 %all-to-all-start.2 = ((bf16[8,512,64]{1,2,0:T(8,128)(2,1)}), bf16[8,512,64]{1,2,0:T(8,128)(2,1)S(1)}, u32[]{:S(2)}, u32[]{:S(2)}) async-start(bf16[8,512,64]{1,2,0:T(8,128)(2,1)} %bitcast.22), calls=%async_computation.2 | async-start | bytes 1048576 | tf_op jit(solution)/shard_map/all_to_all | solution.py:34
  174.4 5.5 %copy-start.1 = (s32[512]{0:T(512)S(1)}, s32[512]{0:T(512)}, u32[]{:S(2)}) copy-start(s32[512]{0:T(512)} %param.10) | copy-start | bytes 6148
  174.4 7.3 %copy-start.2 = (s32[8]{0:T(128)S(1)}, s32[8]{0:T(128)}, u32[]{:S(2)}) copy-start(s32[8]{0:T(128)} %param.11) | copy-start | bytes 100
  174.4 72.4 %all-to-all-start.1 = ((bf16[8,512,512]{2,1,0:T(8,128)(2,1)}), bf16[8,512,512]{2,1,0:T(8,128)(2,1)}, u32[]{:S(2)}, u32[]{:S(2)}) async-start(bf16[8,512,512]{2,1,0:T(8,128)(2,1)} %bitcast.23), calls=%async_computation.1 | async-start | bytes 8388608 | tf_op jit(solution)/shard_map/all_to_all | solution.py:34
  179.6 59.4 %all-gather.5.cloned.1.call-start = ((), (), s32[]{:S(2)}) async-start(), calls=%async_computation.4 | async-start | bytes 2162688 | tf_op jit(solution)/shard_map/all_gather | solution.py:85
Sparse Core Ops, SparseCore 0:
  22.7 107.2 all-gather.2
  183.6 55.3 all-gather.4
where the time goes:
time: 269 us; the launch traced here: 268 us
  waiting for transfers between devices  169 us (63%)
  starting transfers between devices  30.7 us (11%)
  matrix products  27 us (10%)
  local copies, waits for them, and re-layouts  16.5 us (6%)
  between operations  14.2 us (5%)
  other arithmetic  10.6 us (4%)
    all_gather x1, waiting for transfers between devices, body(): gathered = lax.all_gather(normed_rows, ('gx', 'gy'), axis=0, tiled=True)  107 us
    all_gather x1, waiting for transfers between devices, body(): keyval_all = lax.all_gather(keyval_part, ('gx', 'gy'), axis=1, tiled=True)  57.3 us
    all_to_all x2, starting transfers between devices, summed_on_arrival(): lax.all_to_all(in_blocks(value, dim, count), axis, 0, 0, tiled=True)  24.1 us
    dot_general x1, matrix products, body(): jnp.dot(gathered, w_query, preferred_element_type=jnp.float32)  13.7 us
    dot_general x1, matrix products, body(): jnp.dot(gathered, w_keyval, preferred_element_type=jnp.float32)  10.9 us
    all_to_all x1, starting transfers between devices, from_everyone(): return lax.all_to_all(copies, axis, split_axis=0, concat_axis=0, tiled=True)  6.36 us
  transfers between devices with their start and end apart: 5, of which 3 were waited for; matrix products, arithmetic and copies ran while one was open for 9% of the time, Pallas kernels for 0%

commit v1 on v0

v1 whole, which is shorter than its diff:
```python
import functools
import math

import jax
import jax.numpy as jnp
from jax import lax
from jax.experimental import pallas as pl
from jax.experimental.pallas import tpu as pltpu
from jax.sharding import PartitionSpec as P

D = 16384
HD = 128
ROPE_BASE = 500000.0
NORM_EPS = 1e-05
AXES = ("gx", "gy", "gz")


BACK = (0, 2, 3, 1)
GROUPS = ((0,), (1,), (2, 3))

F32 = jnp.float32
BF16 = jnp.bfloat16


def moves(rule):
    pairs = []
    for x in range(4):
        for core in range(2):
            for zh in range(4):
                a, b, c = rule(x, core, zh)
                for k in range(8):
                    target = (((a % 4) * 2 + b) * 4 + c % 4) * 8 + k
                    pairs.append((((x * 2 + core) * 4 + zh) * 8 + k, target))
    return pairs


def send(value, rule):
    return lax.ppermute(value, AXES, moves(rule))


def along_z(step):
    return lambda x, c, zh: (x, c, zh + step)


def along_x(step):
    return lambda x, c, zh: (x + step, c, zh)


def other_core(x, c, zh):
    return (x, 1 - c, zh)


def exchange(value, axis):
    return lax.all_to_all(value, axis, 0, 0, tiled=True)


def gray(v):
    return v ^ (v >> 1)


def spread_kv(kv):
    kv = kv[None]
    steps = (
        lambda x, c, zh: (x, c, zh ^ 1),
        lambda x, c, zh: (x, c, zh ^ 3),
        lambda x, c, zh: (x ^ 1, c, zh),
        lambda x, c, zh: (x ^ 3, c, zh),
        other_core,
    )
    for rule in steps:
        kv = jnp.concatenate([kv, send(kv, rule)])
    return kv


def vmem(count):
    return [pl.BlockSpec(memory_space=pltpu.VMEM)] * count


def smem():
    return pl.BlockSpec(memory_space=pltpu.SMEM)


def prepare_kernel(wq, wk, gain, out):
    width = wq.shape[1]
    g = gain[...]
    for k in range(0, width, 128):
        out[:, k : k + 128] = (wq[:, k : k + 128].astype(F32) * g).astype(BF16)
    kv = (wk[...].astype(F32) * g).astype(BF16)
    out[:, width : width + 64] = kv
    out[:, width + 64 :] = kv


def prepare(wq, wk, gain):
    return pl.pallas_call(
        prepare_kernel,
        out_shape=jax.ShapeDtypeStruct((wq.shape[0], wq.shape[1] + 128), BF16),
        in_specs=vmem(3),
        out_specs=vmem(1)[0],
        cost_estimate=pl.CostEstimate(flops=1 << 20, bytes_accessed=5 << 20, transcendentals=0),
        name="prepare",
    )(wq, wk, gain)


def project_kernel(count, at, *refs):
    parts, (wa, wb, wk), outs = refs[: 4 * count], refs[4 * count : 4 * count + 3], refs[4 * count + 3 : -6]
    rows, a_held, b_held, k_held, row_sems, w_sems = refs[-6:]
    q_out, kv_out = outs[0], outs[-1]
    width = a_held.shape[1]
    base = 2 * width if len(outs) == 1 else 0
    a_copy = pltpu.make_async_copy(wa.at[:, :width], a_held, w_sems.at[0])
    b_copy = pltpu.make_async_copy(wb.at[:, :width], b_held, w_sems.at[1])
    k_copy = pltpu.make_async_copy(wk, k_held, w_sems.at[2])
    a_copy.start()
    row_copies = []
    for p in range(count):
        for i in range(4):
            for core in range(2):
                there = (at[i] * 2 + core) * 64 * count + p * 64
                there = rows.at[pl.ds(pl.multiple_of(there, 64), 64), :]
                here = parts[p * 4 + i].at[core * 64 : (core + 1) * 64, :]
                row_copies.append(pltpu.make_async_copy(here, there, row_sems.at[len(row_copies)]))
    for copy in row_copies:
        copy.start()
    a_copy.wait()
    for copy in row_copies:
        copy.wait()
    b_copy.start()
    k_copy.start()
    size = 256

    def first(i, carry):
        there = pl.ds(pl.multiple_of(i * size, size), size)
        q_out[there, :width] = jnp.dot(rows[there, :], a_held[...], preferred_element_type=F32).astype(BF16)
        for part in range(0, size, 128):
            there = pl.ds(pl.multiple_of(i * size + part, 128), 128)
            squares = jnp.zeros((128, 128), F32)
            for k in range(0, rows.shape[1], 128):
                v = rows[there, k : k + 128].astype(F32)
                squares = squares + v * v
            sums = jnp.broadcast_to(jnp.sum(squares, axis=1, keepdims=True), (128, 128))
            high = sums.astype(BF16).astype(F32)
            lane = lax.broadcasted_iota(jnp.int32, (128, 128), 1)
            kv_out[there, base + 128 : base + 256] = jnp.where(lane < 64, high, sums - high).astype(BF16)
        return carry

    def second(i, carry):
        there = pl.ds(pl.multiple_of(i * size, size), size)
        kv_out[there, base : base + 128] = jnp.dot(
            rows[there, :], k_held[...], preferred_element_type=F32
        ).astype(BF16)
        q_out[there, width : 2 * width] = jnp.dot(
            rows[there, :], b_held[...], preferred_element_type=F32
        ).astype(BF16)
        return carry

    lax.fori_loop(0, rows.shape[0] // size, first, 0)
    b_copy.wait()
    k_copy.wait()
    lax.fori_loop(0, rows.shape[0] // size, second, 0)


def project(at, parts, weights, split):
    depth, width = weights[0].shape[0], weights[0].shape[1] - 128
    widths = (2 * width, 256) if split else (2 * width + 256,)
    count = len(parts) // 4
    return pl.pallas_call(
        functools.partial(project_kernel, count),
        out_shape=tuple(jax.ShapeDtypeStruct((512 * count, v), BF16) for v in widths),
        in_specs=[smem()] + [pl.BlockSpec(memory_space=pl.ANY)] * (4 * count + 3),
        out_specs=tuple(vmem(len(widths))),
        scratch_shapes=[
            pltpu.VMEM((512 * count, depth), BF16),
            pltpu.VMEM((depth, width), BF16),
            pltpu.VMEM((depth, width), BF16),
            pltpu.VMEM((depth, 128), BF16),
            pltpu.SemaphoreType.DMA((8 * count,)),
            pltpu.SemaphoreType.DMA((3,)),
        ],
        cost_estimate=pl.CostEstimate(
            flops=2 * 512 * count * depth * 1152, bytes_accessed=(5 + 3 * count) << 20, transcendentals=0
        ),
    )(at, *parts, *weights)


def turn(v, cosines, sines):
    lane = lax.broadcasted_iota(jnp.int32, v.shape, 1)
    swapped = jnp.where(lane % 2 == 0, pltpu.roll(v, 127, 1), pltpu.roll(v, 1, 1))
    return v * cosines + swapped * sines


def total(ref, lo):
    got = ref[0, :, lo : lo + 128].astype(F32)
    for k in range(1, ref.shape[0]):
        got = got + ref[k, :, lo : lo + 128].astype(F32)
    return got


def factor_of(ref, lo):
    squares = total(ref, lo)
    return lax.rsqrt((squares[:, 0:1] + squares[:, 64:65]) / D + NORM_EPS)


def joined(refs):
    return jnp.concatenate([v[...] for v in refs], axis=0)


def write_q(came, factor, cos, sin, q_own, q_other):
    width = q_own.shape[1]
    cosines, sines = joined(cos) * factor, joined(sin) * factor
    for h in range(2 * width // 128):
        got = turn(total(came, h * 128), cosines, sines).astype(BF16)
        if h * 128 < width:
            q_own[:, h * 128 : (h + 1) * 128] = got
        else:
            q_other[:, h * 128 - width : (h + 1) * 128 - width] = got


def write_kv(came, lo, factor, cos, sin, kv):
    kv[...] = turn(total(came, lo), joined(cos) * factor, joined(sin) * factor).astype(BF16)


def finish_kernel(n, at, came, *refs):
    tables, (q_own, q_other, kv) = [refs[k * n : k * n + n] for k in range(4)], refs[4 * n :]
    base = 2 * q_own.shape[1]
    factor = factor_of(came, base + 128)
    write_q(came, factor, *tables[:2], q_own, q_other)
    write_kv(came, base, factor, *tables[2:], kv)


def finish_kv_kernel(n, at, came, *refs):
    write_kv(came, 0, factor_of(came, 128), refs[:n], refs[n : 2 * n], refs[2 * n])


def finish_q_kernel(n, at, came, came_kv, *refs):
    write_q(came, factor_of(came_kv, 128), refs[:n], refs[n : 2 * n], *refs[2 * n :])


def finish(kernel, rows, came, tables, widths, group):
    block = came[0].shape[1]

    def table(part):
        return pl.BlockSpec((64, 128), lambda n, at: (at[part], 0))

    parts = GROUPS[group]
    return pl.pallas_call(
        functools.partial(kernel, len(parts)),
        out_shape=tuple(jax.ShapeDtypeStruct((block, v), BF16) for v in widths),
        grid_spec=pltpu.PrefetchScalarGridSpec(
            num_scalar_prefetch=1,
            grid=(1,),
            in_specs=[pl.BlockSpec(v.shape, lambda n, at: (0, 0, 0)) for v in came]
            + [table(p) for _ in tables for p in parts],
            out_specs=tuple(pl.BlockSpec((block, v), lambda n, at: (0, 0)) for v in widths),
        ),
        cost_estimate=pl.CostEstimate(flops=1 << 20, bytes_accessed=2 << 20, transcendentals=0),
    )(rows, *came, *[v for v in tables for _ in parts])


def last_kernel(at, pick, q_near, q_far, q_near_came, q_far_came, kv, q_out, kv_out):
    lane = lax.broadcasted_iota(jnp.int32, (64, 128), 1)
    for p in range(4):
        here = slice(p % 2 * 64, p % 2 * 64 + 64)
        rows = pl.ds(pl.multiple_of(at[p] * 64, 64), 64)
        q_out[rows, :] = (q_near, q_far)[p // 2][here, :]
        rows = pl.ds(pl.multiple_of(at[4 + p] * 64, 64), 64)
        q_out[rows, :] = (q_near_came, q_far_came)[p // 2][here, :]
    for s in range(2):
        x_off, odd = pick[4 + 2 * s], pick[5 + 2 * s]
        for t in range(4):
            for core in range(2):

                def part(g, t=t, core=core, x_off=x_off):
                    i = BACK[(t - g) % 4]
                    return kv[pick[8 + core] + x_off + pick[g], i * 64 : (i + 1) * 64, :].astype(F32)

                for half in range(2):
                    a, b = part(2 * half), part(2 * half + 1)
                    low = jnp.where(odd == 0, a, pltpu.roll(a, 64, 1))
                    high = jnp.where(odd == 0, pltpu.roll(b, 64, 1), b)
                    kv_out[s, t * 128 + core * 64 : t * 128 + core * 64 + 64, half * 128 : (half + 1) * 128] = jnp.where(
                        lane < 64, low, high
                    ).astype(BF16)


def last(at, pick, arrays, tokens):
    return pl.pallas_call(
        last_kernel,
        out_shape=(
            jax.ShapeDtypeStruct((tokens, arrays[0].shape[1]), BF16),
            jax.ShapeDtypeStruct((2, tokens, 256), BF16),
        ),
        in_specs=[smem(), smem()] + vmem(len(arrays)),
        out_specs=tuple(vmem(2)),
        cost_estimate=pl.CostEstimate(flops=1 << 10, bytes_accessed=4 << 20, transcendentals=0),
        name="last",
    )(at, pick, *arrays)


def spread_x(v, way):
    left, right = send(v, along_x(1)), send(v, along_x(-1))
    return [v, left, right, send(left if way > 0 else right, along_x(way))]


def body(hidden_rows, norm_gain, w_query, w_keyval, positions, keyval_order):
    gx, gy = (lax.axis_index(a).astype(jnp.int32) for a in AXES[:2])
    x, core = gx // 2, gx % 2
    width = w_query.shape[1]
    tokens = positions.shape[0]

    away = lax.dynamic_slice_in_dim(hidden_rows, (1 - core) * 64, 64, 0)
    home = lax.dynamic_slice_in_dim(hidden_rows, core * 64, 64, 0)
    came = send(away, other_core)
    mine = jnp.where(core == 0, jnp.concatenate([home, came]), jnp.concatenate([came, home]))

    gain = norm_gain.astype(F32)[:, None]
    mine_w = prepare(w_query, w_keyval, gain)
    other_w = send(mine_w, other_core)
    lane = lax.broadcasted_iota(jnp.int32, (1, 128), 1)
    weights = (mine_w, other_w, jnp.where(lane // 64 == core, mine_w[:, width:], other_w[:, width:]))

    def tables(column, is_key):
        inv_freq = jnp.exp((column // 2).astype(F32) * (-2.0 * math.log(ROPE_BASE) / HD))
        angles = positions.astype(F32)[:, None] * inv_freq
        sign = jnp.where(column % 2 == 0, -1.0, 1.0)
        return jnp.where(is_key, jnp.cos(angles), 1.0), jnp.where(is_key, jnp.sin(angles) * sign, 0.0)

    all_tables = (*tables(lane, True), *tables((gy % 2) * 64 + lane % 64, gy < 2))

    ring = jnp.array([0, 3, 1, 2], jnp.int32)
    place = (x + ring) % 4
    source_z = (gy + ring) % 4
    at = jnp.concatenate([source_z * 2 + core, source_z * 2 + 1 - core])
    wanted = lax.dynamic_slice_in_dim(keyval_order, gy * 2, 2, 0)
    four, two = jnp.arange(4, dtype=jnp.int32), jnp.arange(2, dtype=jnp.int32)
    pick = jnp.concatenate(
        [gray(four ^ gy), jnp.stack([gray(wanted // 2 ^ x) * 4, wanted % 2], axis=1).reshape(4), (two ^ core) * 16]
    )

    left, right = send(mine, along_z(1)), send(mine, along_z(-1))
    far = send(left, along_z(1))
    chunks = [spread_x(v, 1 - 2 * (p % 2)) for p, v in enumerate((mine, left, right, far))]
    q_own, q_other, kvs = [], [], []
    for n, group in enumerate(GROUPS):
        split = n + 1 == len(GROUPS)
        sums = project(place, [v for p in group for v in chunks[p]], weights, split)
        sums = [v.reshape(8, v.shape[0] // 8, v.shape[1]) for v in sums]
        if split:
            few = exchange(sums[1], "gz")
            many = exchange(sums[0], "gz")
            (kv,) = finish(finish_kv_kernel, at, (few,), all_tables[2:], (128,), n)
            own, other = finish(finish_q_kernel, at, (many, few), all_tables[:2], (width, width), n)
        else:
            came = exchange(sums[0], "gz")
            own, other, kv = finish(finish_kernel, at, (came,), all_tables, (width, width, 128), n)
        q_own.append(own)
        q_other.append(other)
        kvs.append(kv)
    q_near = jnp.concatenate(q_own[:2])
    q_near_came = send(jnp.concatenate(q_other[:2]), other_core)
    q_far_came = send(q_other[2], other_core)
    kv = spread_kv(jnp.concatenate(kvs))
    return last(at, pick, (q_near, q_own[2], q_near_came, q_far_came, kv), tokens)


def solution(mesh):
    in_specs = (
        P(("gx", "gy"), "gz"),
        P("gz"),
        P("gz", ("gx", "gy")),
        P("gz", ("gx", "gy")),
        P("gz"),
        P(),
    )
    out_specs = (P("gz", ("gx", "gy")), P("gy", "gz", None))

    return jax.shard_map(body, mesh=mesh, in_specs=in_specs, out_specs=out_specs, check_vma=False)
```

time: 269 us -> 268 us (level)
  waiting for transfers between devices: 169 us -> 105 us
  Pallas kernels: 0 us -> 47.2 us
  starting transfers between devices: 30.7 us -> 71.9 us
  matrix products: 27 us -> 0 us
  blocking collectives: 0 us -> 17 us
  between operations: 14.2 us -> 0.93 us
  local copies, waits for them, and re-layouts: 16.5 us -> 12.3 us
    all_gather x2 -> x0, waiting for transfers between devices: 165 us -> none  [the longest x1 107 us: body(): gathered = lax.all_gather(normed_rows, ('gx', 'gy'), axis=0, tiled=True)]
    ppermute x0 -> x24, waiting for transfers between devices: none -> 105 us  [send(): return lax.ppermute(value, AXES, moves(rule))]
    ppermute x0 -> x24, starting transfers between devices: none -> 58.6 us  [send(): return lax.ppermute(value, AXES, moves(rule))]
    pallas_call x0 -> x9, Pallas kernels: none -> 47.2 us  [the longest x3 27.2 us: project(): pl.pallas_call(functools.partial(project_kernel, count), out_shape=tuple(...]
    dot_general x3 -> x0, matrix products: 27 us -> none  [the longest x1 13.7 us: body(): jnp.dot(gathered, w_query, preferred_element_type=jnp.float32)]
    all_to_all x3, starting transfers between devices: 30.5 us -> 13.3 us  [exchange(): return lax.all_to_all(value, axis, 0, 0, tiled=True)]
    all_to_all x0 -> x1, blocking collectives: none -> 17 us  [exchange(): return lax.all_to_all(value, axis, 0, 0, tiled=True)]
    reshape x4 -> x1, local copies, waits for them, and re-layouts: 7.32 us -> 0.08 us  [body(): jnp.stack([gray(wanted // 2 ^ x) * 4, wanted % 2], axis=1).reshape(4)]
  transfers between devices with their start and end apart: 5 -> 27, of which waited for: 3 -> 17; matrix products, arithmetic and copies ran while one was open for 9% -> 6% of each run, Pallas kernels for 0% -> 15%
where the time goes in v1:
time: 268 us; the launch traced here: 266 us
  waiting for transfers between devices  105 us (39%)
  starting transfers between devices  71.9 us (27%)
  Pallas kernels  47.2 us (18%)
  blocking collectives  17 us (6%)
  local copies, waits for them, and re-layouts  12.3 us (5%)
  other arithmetic  12.1 us (5%)
    ppermute x24, waiting for transfers between devices, send(): return lax.ppermute(value, AXES, moves(rule))  105 us
    ppermute x24, starting transfers between devices, send(): return lax.ppermute(value, AXES, moves(rule))  58.6 us
    pallas_call x3, Pallas kernels, project(): pl.pallas_call(functools.partial(project_kernel, count), out_shape=tuple(...  27.2 us
    all_to_all x1, blocking collectives, exchange(): return lax.all_to_all(value, axis, 0, 0, tiled=True)  17 us
    all_to_all x3, starting transfers between devices, exchange(): return lax.all_to_all(value, axis, 0, 0, tiled=True)  13.3 us
    pallas_call x4, Pallas kernels, finish(): pl.pallas_call(functools.partial(kernel, len(parts)), out_shape=tuple((ja...  12.3 us
    unnamed x52, local copies, waits for them, and re-layouts  7.74 us
  transfers between devices with their start and end apart: 27, of which 17 were waited for; matrix products, arithmetic and copies ran while one was open for 6% of the time, Pallas kernels for 15%

profile of v1, /device:TPU:1, one launch (start us, length us, event | category | flops | bytes accessed | tf_op | source)
XLA Modules:
  0.0 266.5 jit_solution(15365038561651611137)
XLA Ops:
  1.3 1.4 copy.13.gain
  2.7 2.0 copy.12.wk
  4.7 4.4 %prepare.1.refs_4_.refs_8_ = bf16[2048,640]{1,0:T(8,128)(2,1)} custom-call(bf16[2048,512]{1,0:T(8,128)(2,1)} %wq.1, bf16[2048,64]{1,0:T(8,128)(2,1)} %copy.12.wk, f32[2048,1]{1,0:T(8,128)} %copy.13.gain), custom_call_target="tpu_custom_call" | custom-call | flops 1048576 | bytes 5242880 | tf_op jit(solution)/shard_map/prepare/pallas_call | solution.py:94
  9.0 3.2 %collective-permute-start.4 = (bf16[2048,640]{1,0:T(8,128)(2,1)}, bf16[2048,640]{1,0:T(8,128)(2,1)S(1)}, u32[]{:S(2)}, u32[]{:S(2)}) collective-permute-start(bf16[2048,640]{1,0:T(8,128)(2,1)} %prepare.1.refs_4_.refs_8_), channel_id=1, source_target_pairs={{0,32},{1,33},{2,34},{3,35},{4,36},{5,37},{6,38},{7,39},{8,40},{9,... | collective-permute-start | bytes 7864328 | tf_op jit(solution)/shard_map/ppermute | solution.py:38
  13.0 4.4 %collective-permute-done = bf16[64,2048]{1,0:T(8,128)(2,1)S(1)} collective-permute-done((bf16[64,2048]{1,0:T(8,128)(2,1)}, bf16[64,2048]{1,0:T(8,128)(2,1)S(1)}, u32[]{:S(2)}, u32[]{:S(2)}) %collective-permute-start) | collective-permute-done | bytes 262176 | tf_op jit(solution)/shard_map/ppermute | solution.py:38
  19.2 1.4 collective-permute-start.5
  20.6 3.1 %collective-permute-start.9 = (bf16[128,2048]{1,0:T(8,128)(2,1)S(1)}, bf16[128,2048]{1,0:T(8,128)(2,1)}, u32[]{:S(2)}, u32[]{:S(2)}) collective-permute-start(bf16[128,2048]{1,0:T(8,128)(2,1)S(1)} %maximum_select_fusion.refs_0_), channel_id=1, source_target_pairs={{0,24},{1,25},{2,26},{3,27},{4,28},{5,29},{6,30},{7,31},{8,0},{9,1... | collective-permute-start | bytes 1572872 | tf_op jit(solution)/shard_map/ppermute | solution.py:38
  23.7 16.2 %collective-permute-done.5.refs_0_ = bf16[128,2048]{1,0:T(8,128)(2,1)S(1)} collective-permute-done((bf16[128,2048]{1,0:T(8,128)(2,1)S(1)}, bf16[128,2048]{1,0:T(8,128)(2,1)S(1)}, u32[]{:S(2)}, u32[]{:S(2)}) %collective-permute-start.5) | collective-permute-done | bytes 524320 | tf_op jit(solution)/shard_map/ppermute | solution.py:38
  39.9 7.3 %collective-permute-start.13 = (bf16[128,2048]{1,0:T(8,128)(2,1)S(1)}, bf16[128,2048]{1,0:T(8,128)(2,1)}, u32[]{:S(2)}, u32[]{:S(2)}) collective-permute-start(bf16[128,2048]{1,0:T(8,128)(2,1)S(1)} %collective-permute-done.5.refs_0_), channel_id=1, source_target_pairs={{0,8},{1,9},{2,10},{3,11},{4,12},{5,13},{6,14},{7,15},{8,16},{9,17... | collective-permute-start | bytes 1572872 | tf_op jit(solution)/shard_map/ppermute | solution.py:38
  48.0 1.2 collective-permute-start.10
  49.3 19.6 %collective-permute-done.13.refs_4_ = bf16[128,2048]{1,0:T(8,128)(2,1)} collective-permute-done((bf16[128,2048]{1,0:T(8,128)(2,1)S(1)}, bf16[128,2048]{1,0:T(8,128)(2,1)}, u32[]{:S(2)}, u32[]{:S(2)}) %collective-permute-start.13) | collective-permute-done | bytes 524320 | tf_op jit(solution)/shard_map/ppermute | solution.py:38
  68.8 2.5 collective-permute-start.15
  73.4 6.7 %collective-permute-done.15.refs_6_ = bf16[128,2048]{1,0:T(8,128)(2,1)} collective-permute-done((bf16[128,2048]{1,0:T(8,128)(2,1)}, bf16[128,2048]{1,0:T(8,128)(2,1)}, u32[]{:S(2)}, u32[]{:S(2)}) %collective-permute-start.15) | collective-permute-done | bytes 524320 | tf_op jit(solution)/shard_map/ppermute | solution.py:38
  80.1 3.4 %collective-permute-start.16 = (bf16[128,2048]{1,0:T(8,128)(2,1)}, bf16[128,2048]{1,0:T(8,128)(2,1)}, u32[]{:S(2)}, u32[]{:S(2)}) collective-permute-start(bf16[128,2048]{1,0:T(8,128)(2,1)} %collective-permute-done.15.refs_6_), channel_id=1, source_target_pairs={{0,192},{1,193},{2,194},{3,195},{4,196},{5,197},{6,198},{7,199},{8... | collective-permute-start | bytes 1572872 | tf_op jit(solution)/shard_map/ppermute | solution.py:38
  83.6 2.4 slice_select_fusion.refs_6_.refs_10_
  86.0 5.3 %collective-permute-done.11.refs_2_ = bf16[128,2048]{1,0:T(8,128)(2,1)} collective-permute-done((bf16[128,2048]{1,0:T(8,128)(2,1)}, bf16[128,2048]{1,0:T(8,128)(2,1)}, u32[]{:S(2)}, u32[]{:S(2)}) %collective-permute-start.11) | collective-permute-done | bytes 524320 | tf_op jit(solution)/shard_map/ppermute | solution.py:38
  91.3 4.0 %collective-permute-done.12.refs_3_ = bf16[128,2048]{1,0:T(8,128)(2,1)} collective-permute-done((bf16[128,2048]{1,0:T(8,128)(2,1)}, bf16[128,2048]{1,0:T(8,128)(2,1)}, u32[]{:S(2)}, u32[]{:S(2)}) %collective-permute-start.12) | collective-permute-done | bytes 524320 | tf_op jit(solution)/shard_map/ppermute | solution.py:38
  95.3 7.2 %collective-permute-done.16.refs_7_ = bf16[128,2048]{1,0:T(8,128)(2,1)} collective-permute-done((bf16[128,2048]{1,0:T(8,128)(2,1)}, bf16[128,2048]{1,0:T(8,128)(2,1)}, u32[]{:S(2)}, u32[]{:S(2)}) %collective-permute-start.16) | collective-permute-done | bytes 524320 | tf_op jit(solution)/shard_map/ppermute | solution.py:38
  102.6 12.0 %shard_map.90 = (bf16[1024,1024]{1,0:T(8,128)(2,1)}, bf16[1024,256]{1,0:T(8,128)(2,1)}) custom-call(s32[4]{0:T(128)} %get-tuple-element.44.at, bf16[128,2048]{1,0:T(8,128)(2,1)} %collective-permute-done.9.refs_0_, bf16[128,2048]{1,0:T(8,128)(2,1)} %collective-permute-done.10.refs_1_, bf16[128,2048]{1,0:T(8,128)(2,1)} %collective-permute-done.11.refs_2_, ...), custom_call_target="tpu_custom_call" | custom-call | flops 4831838208 | bytes 11534336 | tf_op jit(solution)/shard_map/pallas_call | solution.py:166
  114.6 4.8 %all-to-all-start.3 = ((bf16[8,128,256]{2,1,0:T(8,128)(2,1)}), bf16[8,128,256]{2,1,0:T(8,128)(2,1)S(1)}, u32[]{:S(2)}, u32[]{:S(2)}) async-start(bf16[8,128,256]{2,1,0:T(8,128)(2,1)} %bitcast.18), calls=%async_computation.3 | async-start | bytes 1048576 | tf_op jit(solution)/shard_map/all_to_all | solution.py:54
  119.4 3.7 %collective-permute-start.2 = (bf16[128,2048]{1,0:T(8,128)(2,1)S(1)}, bf16[128,2048]{1,0:T(8,128)(2,1)S(1)}, u32[]{:S(2)}, u32[]{:S(2)}) collective-permute-start(bf16[128,2048]{1,0:T(8,128)(2,1)S(1)} %maximum_select_fusion.refs_0_), channel_id=1, source_target_pairs={{0,192},{1,193},{2,194},{3,195},{4,196},{5,197},{6,198},{7,199},{8... | collective-permute-start | bytes 1572872 | tf_op jit(solution)/shard_map/ppermute | solution.py:38
  123.1 7.9 %collective-permute-done.2.refs_2_ = bf16[128,2048]{1,0:T(8,128)(2,1)S(1)} collective-permute-done((bf16[128,2048]{1,0:T(8,128)(2,1)S(1)}, bf16[128,2048]{1,0:T(8,128)(2,1)S(1)}, u32[]{:S(2)}, u32[]{:S(2)}) %collective-permute-start.2) | collective-permute-done | bytes 524320 | tf_op jit(solution)/shard_map/ppermute | solution.py:38
  131.0 3.3 %collective-permute-done.3.refs_3_ = bf16[128,2048]{1,0:T(8,128)(2,1)S(1)} collective-permute-done((bf16[128,2048]{1,0:T(8,128)(2,1)}, bf16[128,2048]{1,0:T(8,128)(2,1)S(1)}, u32[]{:S(2)}, u32[]{:S(2)}) %collective-permute-start.3) | collective-permute-done | bytes 524320 | tf_op jit(solution)/shard_map/ppermute | solution.py:38
  135.1 7.6 %shard_map.86 = bf16[512,1280]{1,0:T(8,128)(2,1)} custom-call(s32[4]{0:T(128)} %get-tuple-element.44.at, bf16[128,2048]{1,0:T(8,128)(2,1)} %copy-done.4, bf16[128,2048]{1,0:T(8,128)(2,1)} %collective-permute-done.1.refs_1_, bf16[128,2048]{1,0:T(8,128)(2,1)} %copy-done.9, bf16[128,2048]{1,0:T(8,128)(2,1)} %copy-done.10, ...), custom_call_target="tpu_custom_call" | custom-call | flops 2415919104 | bytes 8388608 | tf_op jit(solution)/shard_map/pallas_call | solution.py:166
  142.8 4.7 %all-to-all-start = ((bf16[8,64,1280]{2,1,0:T(8,128)(2,1)}), bf16[8,64,1280]{2,1,0:T(8,128)(2,1)S(1)}, u32[]{:S(2)}, u32[]{:S(2)}) async-start(bf16[8,64,1280]{2,1,0:T(8,128)(2,1)} %bitcast.15), calls=%async_computation | async-start | bytes 2621440 | tf_op jit(solution)/shard_map/all_to_all | solution.py:54
  149.1 7.0 %collective-permute-done.7.refs_2_ = bf16[128,2048]{1,0:T(8,128)(2,1)S(1)} collective-permute-done((bf16[128,2048]{1,0:T(8,128)(2,1)S(1)}, bf16[128,2048]{1,0:T(8,128)(2,1)S(1)}, u32[]{:S(2)}, u32[]{:S(2)}) %collective-permute-start.7) | collective-permute-done | bytes 524320 | tf_op jit(solution)/shard_map/ppermute | solution.py:38
  156.1 2.3 collective-permute-start.8
  158.4 8.6 %collective-permute-done.8.refs_3_ = bf16[128,2048]{1,0:T(8,128)(2,1)} collective-permute-done((bf16[128,2048]{1,0:T(8,128)(2,1)S(1)}, bf16[128,2048]{1,0:T(8,128)(2,1)}, u32[]{:S(2)}, u32[]{:S(2)}) %collective-permute-start.8) | collective-permute-done | bytes 524320 | tf_op jit(solution)/shard_map/ppermute | solution.py:38
  167.0 7.6 %shard_map.88 = bf16[512,1280]{1,0:T(8,128)(2,1)} custom-call(s32[4]{0:T(128)} %get-tuple-element.44.at, bf16[128,2048]{1,0:T(8,128)(2,1)} %copy-done.5, bf16[128,2048]{1,0:T(8,128)(2,1)} %copy-done.8, bf16[128,2048]{1,0:T(8,128)(2,1)} %copy-done.7, bf16[128,2048]{1,0:T(8,128)(2,1)} %collective-permute-done.8.refs_3_, ...), custom_call_target="tpu_custom_call" | custom-call | flops 2415919104 | bytes 8388608 | tf_op jit(solution)/shard_map/pallas_call | solution.py:166
  174.6 17.0 %all_to_all.20.came = bf16[8,64,1280]{2,1,0:T(8,128)(2,1)} all-to-all(bf16[8,64,1280]{2,1,0:T(8,128)(2,1)} %bitcast.16), channel_id=1, replica_groups=mesh['gx'=8,'gy'=4,'gz'=8] {'gz'}, dimensions={0} | all-to-all | bytes 2621440 | tf_op jit(solution)/shard_map/all_to_all | solution.py:54
  191.7 3.7 %all-to-all-start.2 = ((bf16[8,128,1024]{2,1,0:T(8,128)(2,1)}), bf16[8,128,1024]{2,1,0:T(8,128)(2,1)S(1)}, u32[]{:S(2)}, u32[]{:S(2)}) async-start(bf16[8,128,1024]{2,1,0:T(8,128)(2,1)} %bitcast.17), calls=%async_computation.2 | async-start | bytes 4194304 | tf_op jit(solution)/shard_map/all_to_all | solution.py:54
  196.2 3.0 %fusion.3 = (f32[512,128]{1,0:T(8,128)}, f32[512,128]{1,0:T(8,128)}, f32[512,128]{1,0:T(8,128)}, f32[512,128]{1,0:T(8,128)}) fusion(f32[128]{0:T(128)S(1)} %get-tuple-element.45, f32[128]{0:T(128)S(1)} %get-tuple-element.48, f32[512]{0:T(512)S(1)} %convert_element_type.21, pred[]{:T(512)S(6)} %lt.60, f32[128]{0:T(128)S(1)} %get-tuple-element.47, ...), kind=kLoop, calls=%fused_computation.10 | loop fusion | flops 393216 | bytes 1052673 | tf_op jit(solution)/shard_map/jit(_where)/select_n | solution.py:325
  199.2 2.5 shard_map.92
  201.7 3.0 %shard_map.87 = (bf16[64,512]{1,0:T(8,128)(2,1)}, bf16[64,512]{1,0:T(8,128)(2,1)}, bf16[64,128]{1,0:T(8,128)(2,1)}) custom-call(s32[8]{0:T(128)} %pad_add_fusion.1.at, bf16[8,64,1280]{2,1,0:T(8,128)(2,1)} %copy-done.2, f32[512,128]{1,0:T(8,128)} %get-tuple-element.42.refs_0_.refs_1_, f32[512,128]{1,0:T(8,128)} %get-tuple-element.43.refs_1_.refs_2_.refs_3_, ...), custom_call_target="tpu_custom_call" | custom-call | flops 1048576 | bytes 2097152 | tf_op jit(solution)/shard_map/pallas_call | solution.py:245
  204.8 3.0 %shard_map.89 = (bf16[64,512]{1,0:T(8,128)(2,1)}, bf16[64,512]{1,0:T(8,128)(2,1)}, bf16[64,128]{1,0:T(8,128)(2,1)}) custom-call(s32[8]{0:T(128)} %pad_add_fusion.1.at, bf16[8,64,1280]{2,1,0:T(8,128)(2,1)} %all_to_all.20.came, f32[512,128]{1,0:T(8,128)} %get-tuple-element.42.refs_0_.refs_1_, f32[512,128]{1,0:T(8,128)} %get-tuple-element.43.refs_1_.refs_2_.refs_3_, ...), custom_call_target="tpu_custom_call" | custom-call | flops 1048576 | bytes 2097152 | tf_op jit(solution)/shard_map/pallas_call | solution.py:245
  208.6 5.5 %collective-permute-start.19 = (bf16[1,256,128]{2,1,0:T(8,128)(2,1)S(1)}, bf16[1,256,128]{2,1,0:T(8,128)(2,1)S(1)}, u32[]{:S(2)}, u32[]{:S(2)}) collective-permute-start(bf16[1,256,128]{2,1,0:T(8,128)(2,1)S(1)} %maximum_bitcast_fusion), channel_id=1, source_target_pairs={{0,8},{1,9},{2,10},{3,11},{4,12},{5,13},{6,14},{7,15},{8,0},{9,1},... | collective-permute-start | bytes 196616 | tf_op jit(solution)/shard_map/ppermute | solution.py:38
  214.0 1.9 collective-permute-done.19
  216.0 6.6 %collective-permute-start.20 = (bf16[2,256,128]{2,1,0:T(8,128)(2,1)S(1)}, bf16[2,256,128]{2,1,0:T(8,128)(2,1)S(1)}, u32[]{:S(2)}, u32[]{:S(2)}) collective-permute-start(bf16[2,256,128]{2,1,0:T(8,128)(2,1)S(1)} %pad_maximum_fusion.4), channel_id=1, source_target_pairs={{0,24},{1,25},{2,26},{3,27},{4,28},{5,29},{6,30},{7,31},{8,16},{9,... | collective-permute-start | bytes 393224 | tf_op jit(solution)/shard_map/ppermute | solution.py:38
  222.6 3.8 %collective-permute-done.20 = bf16[2,256,128]{2,1,0:T(8,128)(2,1)S(1)} collective-permute-done((bf16[2,256,128]{2,1,0:T(8,128)(2,1)S(1)}, bf16[2,256,128]{2,1,0:T(8,128)(2,1)S(1)}, u32[]{:S(2)}, u32[]{:S(2)}) %collective-permute-start.20) | collective-permute-done | bytes 131104 | tf_op jit(solution)/shard_map/ppermute | solution.py:38
  226.6 5.2 %collective-permute-done.21 = bf16[4,256,128]{2,1,0:T(8,128)(2,1)S(1)} collective-permute-done((bf16[4,256,128]{2,1,0:T(8,128)(2,1)S(1)}, bf16[4,256,128]{2,1,0:T(8,128)(2,1)S(1)}, u32[]{:S(2)}, u32[]{:S(2)}) %collective-permute-start.21) | collective-permute-done | bytes 262176 | tf_op jit(solution)/shard_map/ppermute | solution.py:38
  231.8 3.0 %collective-permute-start.22 = (bf16[8,256,128]{2,1,0:T(8,128)(2,1)S(1)}, bf16[8,256,128]{2,1,0:T(8,128)(2,1)S(1)}, u32[]{:S(2)}, u32[]{:S(2)}) collective-permute-start(bf16[8,256,128]{2,1,0:T(8,128)(2,1)S(1)} %pad_maximum_fusion), channel_id=1, source_target_pairs={{0,192},{1,193},{2,194},{3,195},{4,196},{5,197},{6,198},{7,199},{8... | collective-permute-start | bytes 1572872 | tf_op jit(solution)/shard_map/ppermute | solution.py:38
  234.8 1.4 constant_dynamic-update-slice_fusion.4
  238.4 2.9 %collective-permute-done.22 = bf16[8,256,128]{2,1,0:T(8,128)(2,1)S(1)} collective-permute-done((bf16[8,256,128]{2,1,0:T(8,128)(2,1)S(1)}, bf16[8,256,128]{2,1,0:T(8,128)(2,1)S(1)}, u32[]{:S(2)}, u32[]{:S(2)}) %collective-permute-start.22) | collective-permute-done | bytes 524320 | tf_op jit(solution)/shard_map/ppermute | solution.py:38
  241.4 1.2 constant_dynamic-update-slice_fusion
  242.6 11.6 %collective-permute-start.23 = (bf16[16,256,128]{2,1,0:T(8,128)(2,1)}, bf16[16,256,128]{2,1,0:T(8,128)(2,1)S(1)}, u32[]{:S(2)}, u32[]{:S(2)}) collective-permute-start(bf16[16,256,128]{2,1,0:T(8,128)(2,1)} %get-tuple-element.26), channel_id=1, source_target_pairs={{0,32},{1,33},{2,34},{3,35},{4,36},{5,37},{6,38},{7,39},{8,40},{9,... | collective-permute-start | bytes 3145736 | tf_op jit(solution)/shard_map/ppermute | solution.py:38
  255.9 1.3 copy-done.1
  257.2 3.7 %shard_map.91 = (bf16[128,512]{1,0:T(8,128)(2,1)}, bf16[128,512]{1,0:T(8,128)(2,1)}) custom-call(s32[8]{0:T(128)} %pad_add_fusion.1.at, bf16[8,128,1024]{2,1,0:T(8,128)(2,1)} %copy-done.1, bf16[8,128,256]{2,1,0:T(8,128)(2,1)} %copy-done.3, f32[512,128]{1,0:T(8,128)} %get-tuple-element.42.refs_0_.refs_1_, f32[512,128]{1,0:T(8,128)} %get-tuple-element.42.refs_0_.refs_1_, ...), custom_call_target="tpu_custom_call" | custom-call | flops 1048576 | bytes 2097152 | tf_op jit(solution)/shard_map/pallas_call | solution.py:245
  263.2 3.2 %last.1 = (bf16[512,512]{1,0:T(8,128)(2,1)}, bf16[2,512,256]{2,1,0:T(8,128)(2,1)}) custom-call(s32[8]{0:T(128)} %pad_add_fusion.1.at, s32[10]{0:T(128)} %pad_add_fusion.2.pick, bf16[128,512]{1,0:T(8,128)(2,1)} %pad_maximum_fusion.2.q_near, bf16[128,512]{1,0:T(8,128)(2,1)} %get-tuple-element.16.q_far, bf16[128,512]{1,0:T(8,128)(2,1)} %copy-done.14, ...), custom_call_target="tpu_custom_call" | custom-call | flops 1024 | bytes 4194304 | tf_op jit(solution)/shard_map/last/pallas_call | solution.py:286
  (98 shorter events, 16.5 us)
Async XLA Ops:
  4.7 7.6 %copy-start.11 = (bf16[128,2048]{1,0:T(8,128)(2,1)S(1)}, bf16[128,2048]{1,0:T(8,128)(2,1)}, u32[]{:S(2)}) copy-start(bf16[128,2048]{1,0:T(8,128)(2,1)} %param.7) | copy-start | bytes 1572868
  9.0 62.3 %copy-start.23 = (s32[4]{0:T(128)S(1)}, s32[4]{0:T(128)}, u32[]{:S(2)}) copy-start(s32[4]{0:T(128)} %constant.153.clone) | copy-start | bytes 52
  9.0 74.5 %collective-permute-start.4 = (bf16[2048,640]{1,0:T(8,128)(2,1)}, bf16[2048,640]{1,0:T(8,128)(2,1)S(1)}, u32[]{:S(2)}, u32[]{:S(2)}) collective-permute-start(bf16[2048,640]{1,0:T(8,128)(2,1)} %prepare.1.refs_4_.refs_8_), channel_id=1, source_target_pairs={{0,32},{1,33},{2,34},{3,35},{4,36},{5,37},{6,38},{7,39},{8,40},{9,... | collective-permute-start | bytes 7864328 | tf_op jit(solution)/shard_map/ppermute | solution.py:38
  13.0 4.4 %collective-permute-start = (bf16[64,2048]{1,0:T(8,128)(2,1)}, bf16[64,2048]{1,0:T(8,128)(2,1)S(1)}, u32[]{:S(2)}, u32[]{:S(2)}) collective-permute-start(bf16[64,2048]{1,0:T(8,128)(2,1)} %get-tuple-element.29), channel_id=1, source_target_pairs={{0,32},{1,33},{2,34},{3,35},{4,36},{5,37},{6,38},{7,39},{8,40},{9,... | collective-permute-start | bytes 786440 | tf_op jit(solution)/shard_map/ppermute | solution.py:38
  19.2 100.2 %copy-start.4 = (bf16[128,2048]{1,0:T(8,128)(2,1)}, bf16[128,2048]{1,0:T(8,128)(2,1)S(1)}, u32[]{:S(2)}) copy-start(bf16[128,2048]{1,0:T(8,128)(2,1)S(1)} %maximum_select_fusion.refs_0_) | copy-start | bytes 1572868
  19.2 20.7 %collective-permute-start.5 = (bf16[128,2048]{1,0:T(8,128)(2,1)S(1)}, bf16[128,2048]{1,0:T(8,128)(2,1)S(1)}, u32[]{:S(2)}, u32[]{:S(2)}) collective-permute-start(bf16[128,2048]{1,0:T(8,128)(2,1)S(1)} %maximum_select_fusion.refs_0_), channel_id=1, source_target_pairs={{0,8},{1,9},{2,10},{3,11},{4,12},{5,13},{6,14},{7,15},{8,16},{9,17... | collective-permute-start | bytes 1572872 | tf_op jit(solution)/shard_map/ppermute | solution.py:38
  20.6 27.5 %collective-permute-start.9 = (bf16[128,2048]{1,0:T(8,128)(2,1)S(1)}, bf16[128,2048]{1,0:T(8,128)(2,1)}, u32[]{:S(2)}, u32[]{:S(2)}) collective-permute-start(bf16[128,2048]{1,0:T(8,128)(2,1)S(1)} %maximum_select_fusion.refs_0_), channel_id=1, source_target_pairs={{0,24},{1,25},{2,26},{3,27},{4,28},{5,29},{6,30},{7,31},{8,0},{9,1... | collective-permute-start | bytes 1572872 | tf_op jit(solution)/shard_map/ppermute | solution.py:38
  39.9 8.1 %copy-start.5 = (bf16[128,2048]{1,0:T(8,128)(2,1)}, bf16[128,2048]{1,0:T(8,128)(2,1)S(1)}, u32[]{:S(2)}) copy-start(bf16[128,2048]{1,0:T(8,128)(2,1)S(1)} %collective-permute-done.5.refs_0_) | copy-start | bytes 1572868
  39.9 28.9 %collective-permute-start.13 = (bf16[128,2048]{1,0:T(8,128)(2,1)S(1)}, bf16[128,2048]{1,0:T(8,128)(2,1)}, u32[]{:S(2)}, u32[]{:S(2)}) collective-permute-start(bf16[128,2048]{1,0:T(8,128)(2,1)S(1)} %collective-permute-done.5.refs_0_), channel_id=1, source_target_pairs={{0,8},{1,9},{2,10},{3,11},{4,12},{5,13},{6,14},{7,15},{8,16},{9,17... | collective-permute-start | bytes 1572872 | tf_op jit(solution)/shard_map/ppermute | solution.py:38
  48.0 25.3 %collective-permute-start.10 = (bf16[128,2048]{1,0:T(8,128)(2,1)}, bf16[128,2048]{1,0:T(8,128)(2,1)}, u32[]{:S(2)}, u32[]{:S(2)}) collective-permute-start(bf16[128,2048]{1,0:T(8,128)(2,1)} %collective-permute-done.9.refs_0_), channel_id=1, source_target_pairs={{0,64},{1,65},{2,66},{3,67},{4,68},{5,69},{6,70},{7,71},{8,72},{9,... | collective-permute-start | bytes 1572872 | tf_op jit(solution)/shard_map/ppermute | solution.py:38
  68.8 11.3 %collective-permute-start.15 = (bf16[128,2048]{1,0:T(8,128)(2,1)}, bf16[128,2048]{1,0:T(8,128)(2,1)}, u32[]{:S(2)}, u32[]{:S(2)}) collective-permute-start(bf16[128,2048]{1,0:T(8,128)(2,1)} %collective-permute-done.13.refs_4_), channel_id=1, source_target_pairs={{0,192},{1,193},{2,194},{3,195},{4,196},{5,197},{6,198},{7,199},{8... | collective-permute-start | bytes 1572872 | tf_op jit(solution)/shard_map/ppermute | solution.py:38
  71.9 19.4 %collective-permute-start.11 = (bf16[128,2048]{1,0:T(8,128)(2,1)}, bf16[128,2048]{1,0:T(8,128)(2,1)}, u32[]{:S(2)}, u32[]{:S(2)}) collective-permute-start(bf16[128,2048]{1,0:T(8,128)(2,1)} %collective-permute-done.9.refs_0_), channel_id=1, source_target_pairs={{0,192},{1,193},{2,194},{3,195},{4,196},{5,197},{6,198},{7,199},{8... | collective-permute-start | bytes 1572872 | tf_op jit(solution)/shard_map/ppermute | solution.py:38
  72.5 22.9 %collective-permute-start.14 = (bf16[128,2048]{1,0:T(8,128)(2,1)}, bf16[128,2048]{1,0:T(8,128)(2,1)}, u32[]{:S(2)}, u32[]{:S(2)}) collective-permute-start(bf16[128,2048]{1,0:T(8,128)(2,1)} %collective-permute-done.13.refs_4_), channel_id=1, source_target_pairs={{0,64},{1,65},{2,66},{3,67},{4,68},{5,69},{6,70},{7,71},{8,72},{9,... | collective-permute-start | bytes 1572872 | tf_op jit(solution)/shard_map/ppermute | solution.py:38
  73.4 21.9 %collective-permute-start.12 = (bf16[128,2048]{1,0:T(8,128)(2,1)}, bf16[128,2048]{1,0:T(8,128)(2,1)}, u32[]{:S(2)}, u32[]{:S(2)}) collective-permute-start(bf16[128,2048]{1,0:T(8,128)(2,1)} %collective-permute-done.10.refs_1_), channel_id=1, source_target_pairs={{0,64},{1,65},{2,66},{3,67},{4,68},{5,69},{6,70},{7,71},{8,72},{9,... | collective-permute-start | bytes 1572872 | tf_op jit(solution)/shard_map/ppermute | solution.py:38
  80.1 22.5 %collective-permute-start.16 = (bf16[128,2048]{1,0:T(8,128)(2,1)}, bf16[128,2048]{1,0:T(8,128)(2,1)}, u32[]{:S(2)}, u32[]{:S(2)}) collective-permute-start(bf16[128,2048]{1,0:T(8,128)(2,1)} %collective-permute-done.15.refs_6_), channel_id=1, source_target_pairs={{0,192},{1,193},{2,194},{3,195},{4,196},{5,197},{6,198},{7,199},{8... | collective-permute-start | bytes 1572872 | tf_op jit(solution)/shard_map/ppermute | solution.py:38
  83.5 19.1 %copy-start = (bf16[2048,640]{1,0:T(8,128)(2,1)}, bf16[2048,640]{1,0:T(8,128)(2,1)S(1)}, u32[]{:S(2)}) copy-start(bf16[2048,640]{1,0:T(8,128)(2,1)S(1)} %collective-permute-done.4.refs_5_.refs_9_) | copy-start | bytes 7864324
  83.5 39.6 %collective-permute-start.1 = (bf16[128,2048]{1,0:T(8,128)(2,1)S(1)}, bf16[128,2048]{1,0:T(8,128)(2,1)}, u32[]{:S(2)}, u32[]{:S(2)}) collective-permute-start(bf16[128,2048]{1,0:T(8,128)(2,1)S(1)} %maximum_select_fusion.refs_0_), channel_id=1, source_target_pairs={{0,64},{1,65},{2,66},{3,67},{4,68},{5,69},{6,70},{7,71},{8,72},{9,... | collective-permute-start | bytes 1572872 | tf_op jit(solution)/shard_map/ppermute | solution.py:38
  114.6 28.2 %all-to-all-start.3 = ((bf16[8,128,256]{2,1,0:T(8,128)(2,1)}), bf16[8,128,256]{2,1,0:T(8,128)(2,1)S(1)}, u32[]{:S(2)}, u32[]{:S(2)}) async-start(bf16[8,128,256]{2,1,0:T(8,128)(2,1)} %bitcast.18), calls=%async_computation.3 | async-start | bytes 1048576 | tf_op jit(solution)/shard_map/all_to_all | solution.py:54
  119.4 11.6 %collective-permute-start.2 = (bf16[128,2048]{1,0:T(8,128)(2,1)S(1)}, bf16[128,2048]{1,0:T(8,128)(2,1)S(1)}, u32[]{:S(2)}, u32[]{:S(2)}) collective-permute-start(bf16[128,2048]{1,0:T(8,128)(2,1)S(1)} %maximum_select_fusion.refs_0_), channel_id=1, source_target_pairs={{0,192},{1,193},{2,194},{3,195},{4,196},{5,197},{6,198},{7,199},{8... | collective-permute-start | bytes 1572872 | tf_op jit(solution)/shard_map/ppermute | solution.py:38
  123.1 11.3 %collective-permute-start.3 = (bf16[128,2048]{1,0:T(8,128)(2,1)}, bf16[128,2048]{1,0:T(8,128)(2,1)S(1)}, u32[]{:S(2)}, u32[]{:S(2)}) collective-permute-start(bf16[128,2048]{1,0:T(8,128)(2,1)} %collective-permute-done.1.refs_1_), channel_id=1, source_target_pairs={{0,64},{1,65},{2,66},{3,67},{4,68},{5,69},{6,70},{7,71},{8,72},{9,... | collective-permute-start | bytes 1572872 | tf_op jit(solution)/shard_map/ppermute | solution.py:38
  131.0 3.3 %copy-start.9 = (bf16[128,2048]{1,0:T(8,128)(2,1)}, bf16[128,2048]{1,0:T(8,128)(2,1)S(1)}, u32[]{:S(2)}) copy-start(bf16[128,2048]{1,0:T(8,128)(2,1)S(1)} %collective-permute-done.2.refs_2_) | copy-start | bytes 1572868
  134.4 0.8 copy-start.10
  142.8 4.8 %copy-start.6 = (bf16[128,2048]{1,0:T(8,128)(2,1)S(1)}, bf16[128,2048]{1,0:T(8,128)(2,1)}, u32[]{:S(2)}) copy-start(bf16[128,2048]{1,0:T(8,128)(2,1)} %copy-done.5) | copy-start | bytes 1572868
  142.8 31.8 %copy-start.3 = (bf16[8,128,256]{2,1,0:T(8,128)(2,1)}, bf16[8,128,256]{2,1,0:T(8,128)(2,1)S(1)}, u32[]{:S(2)}) copy-start(bf16[8,128,256]{2,1,0:T(8,128)(2,1)S(1)} %all-to-all-done.3.came_kv.came) | copy-start | bytes 1572868
  142.8 31.8 %all-to-all-start = ((bf16[8,64,1280]{2,1,0:T(8,128)(2,1)}), bf16[8,64,1280]{2,1,0:T(8,128)(2,1)S(1)}, u32[]{:S(2)}, u32[]{:S(2)}) async-start(bf16[8,64,1280]{2,1,0:T(8,128)(2,1)} %bitcast.15), calls=%async_computation | async-start | bytes 2621440 | tf_op jit(solution)/shard_map/all_to_all | solution.py:54
  147.5 8.5 %collective-permute-start.7 = (bf16[128,2048]{1,0:T(8,128)(2,1)S(1)}, bf16[128,2048]{1,0:T(8,128)(2,1)S(1)}, u32[]{:S(2)}, u32[]{:S(2)}) collective-permute-start(bf16[128,2048]{1,0:T(8,128)(2,1)S(1)} %copy-done.6), channel_id=1, source_target_pairs={{0,192},{1,193},{2,194},{3,195},{4,196},{5,197},{6,198},{7,199},{8... | collective-permute-start | bytes 1572872 | tf_op jit(solution)/shard_map/ppermute | solution.py:38
  148.5 9.9 %collective-permute-start.6 = (bf16[128,2048]{1,0:T(8,128)(2,1)S(1)}, bf16[128,2048]{1,0:T(8,128)(2,1)S(1)}, u32[]{:S(2)}, u32[]{:S(2)}) collective-permute-start(bf16[128,2048]{1,0:T(8,128)(2,1)S(1)} %copy-done.6), channel_id=1, source_target_pairs={{0,64},{1,65},{2,66},{3,67},{4,68},{5,69},{6,70},{7,71},{8,72},{9,... | collective-permute-start | bytes 1572872 | tf_op jit(solution)/shard_map/ppermute | solution.py:38
  156.1 10.9 %copy-start.7 = (bf16[128,2048]{1,0:T(8,128)(2,1)}, bf16[128,2048]{1,0:T(8,128)(2,1)S(1)}, u32[]{:S(2)}) copy-start(bf16[128,2048]{1,0:T(8,128)(2,1)S(1)} %collective-permute-done.7.refs_2_) | copy-start | bytes 1572868
  156.1 10.9 %collective-permute-start.8 = (bf16[128,2048]{1,0:T(8,128)(2,1)S(1)}, bf16[128,2048]{1,0:T(8,128)(2,1)}, u32[]{:S(2)}, u32[]{:S(2)}) collective-permute-start(bf16[128,2048]{1,0:T(8,128)(2,1)S(1)} %collective-permute-done.7.refs_2_), channel_id=1, source_target_pairs={{0,192},{1,193},{2,194},{3,195},{4,196},{5,197},{6,198},{7,199},{8... | collective-permute-start | bytes 1572872 | tf_op jit(solution)/shard_map/ppermute | solution.py:38
  158.4 8.6 %copy-start.8 = (bf16[128,2048]{1,0:T(8,128)(2,1)}, bf16[128,2048]{1,0:T(8,128)(2,1)S(1)}, u32[]{:S(2)}) copy-start(bf16[128,2048]{1,0:T(8,128)(2,1)S(1)} %collective-permute-done.6.refs_1_) | copy-start | bytes 1572868
  174.6 17.1 %copy-start.2 = (bf16[8,64,1280]{2,1,0:T(8,128)(2,1)}, bf16[8,64,1280]{2,1,0:T(8,128)(2,1)S(1)}, u32[]{:S(2)}) copy-start(bf16[8,64,1280]{2,1,0:T(8,128)(2,1)S(1)} %all-to-all-done.came) | copy-start | bytes 3932164
  191.7 3.8 %copy-start.21 = (s32[512]{0:T(512)S(1)}, s32[512]{0:T(512)}, u32[]{:S(2)}) copy-start(s32[512]{0:T(512)} %param.11) | copy-start | bytes 6148
  191.7 64.2 %all-to-all-start.2 = ((bf16[8,128,1024]{2,1,0:T(8,128)(2,1)}), bf16[8,128,1024]{2,1,0:T(8,128)(2,1)S(1)}, u32[]{:S(2)}, u32[]{:S(2)}) async-start(bf16[8,128,1024]{2,1,0:T(8,128)(2,1)} %bitcast.17), calls=%async_computation.2 | async-start | bytes 4194304 | tf_op jit(solution)/shard_map/all_to_all | solution.py:54
  201.7 6.1 %copy-start.12 = (bf16[128,128]{1,0:T(8,128)(2,1)S(1)}, bf16[128,128]{1,0:T(8,128)(2,1)}, u32[]{:S(2)}) copy-start(bf16[128,128]{1,0:T(8,128)(2,1)} %shard_map.92) | copy-start | bytes 98308
  204.8 3.0 %copy-start.20 = (bf16[64,128]{1,0:T(8,128)(2,1)S(1)}, bf16[64,128]{1,0:T(8,128)(2,1)}, u32[]{:S(2)}) copy-start(bf16[64,128]{1,0:T(8,128)(2,1)} %get-tuple-element.20) | copy-start | bytes 49156
  208.6 7.4 %collective-permute-start.19 = (bf16[1,256,128]{2,1,0:T(8,128)(2,1)S(1)}, bf16[1,256,128]{2,1,0:T(8,128)(2,1)S(1)}, u32[]{:S(2)}, u32[]{:S(2)}) collective-permute-start(bf16[1,256,128]{2,1,0:T(8,128)(2,1)S(1)} %maximum_bitcast_fusion), channel_id=1, source_target_pairs={{0,8},{1,9},{2,10},{3,11},{4,12},{5,13},{6,14},{7,15},{8,0},{9,1},... | collective-permute-start | bytes 196616 | tf_op jit(solution)/shard_map/ppermute | solution.py:38
  216.0 10.4 %collective-permute-start.20 = (bf16[2,256,128]{2,1,0:T(8,128)(2,1)S(1)}, bf16[2,256,128]{2,1,0:T(8,128)(2,1)S(1)}, u32[]{:S(2)}, u32[]{:S(2)}) collective-permute-start(bf16[2,256,128]{2,1,0:T(8,128)(2,1)S(1)} %pad_maximum_fusion.4), channel_id=1, source_target_pairs={{0,24},{1,25},{2,26},{3,27},{4,28},{5,29},{6,30},{7,31},{8,16},{9,... | collective-permute-start | bytes 393224 | tf_op jit(solution)/shard_map/ppermute | solution.py:38
  226.4 27.8 %copy-start.22 = (s32[8]{0:T(128)S(1)}, s32[8]{0:T(128)}, u32[]{:S(2)}) copy-start(s32[8]{0:T(128)} %param.12) | copy-start | bytes 100
  226.4 28.6 %copy-start.18 = (bf16[64,512]{1,0:T(8,128)(2,1)S(1)}, bf16[64,512]{1,0:T(8,128)(2,1)}, u32[]{:S(2)}) copy-start(bf16[64,512]{1,0:T(8,128)(2,1)} %get-tuple-element.17) | copy-start | bytes 196612
  226.4 28.6 %copy-start.19 = (bf16[64,512]{1,0:T(8,128)(2,1)S(1)}, bf16[64,512]{1,0:T(8,128)(2,1)}, u32[]{:S(2)}) copy-start(bf16[64,512]{1,0:T(8,128)(2,1)} %get-tuple-element.18) | copy-start | bytes 196612
  226.5 28.7 %copy-start.16 = (bf16[64,512]{1,0:T(8,128)(2,1)S(1)}, bf16[64,512]{1,0:T(8,128)(2,1)}, u32[]{:S(2)}) copy-start(bf16[64,512]{1,0:T(8,128)(2,1)} %get-tuple-element.12) | copy-start | bytes 196612
  226.5 28.7 %copy-start.17 = (bf16[64,512]{1,0:T(8,128)(2,1)S(1)}, bf16[64,512]{1,0:T(8,128)(2,1)}, u32[]{:S(2)}) copy-start(bf16[64,512]{1,0:T(8,128)(2,1)} %get-tuple-element.13) | copy-start | bytes 196612
  226.5 5.3 %collective-permute-start.21 = (bf16[4,256,128]{2,1,0:T(8,128)(2,1)S(1)}, bf16[4,256,128]{2,1,0:T(8,128)(2,1)S(1)}, u32[]{:S(2)}, u32[]{:S(2)}) collective-permute-start(bf16[4,256,128]{2,1,0:T(8,128)(2,1)S(1)} %pad_maximum_fusion.1), channel_id=1, source_target_pairs={{0,64},{1,65},{2,66},{3,67},{4,68},{5,69},{6,70},{7,71},{8,72},{9,... | collective-permute-start | bytes 786440 | tf_op jit(solution)/shard_map/ppermute | solution.py:38
  231.8 9.5 %collective-permute-start.22 = (bf16[8,256,128]{2,1,0:T(8,128)(2,1)S(1)}, bf16[8,256,128]{2,1,0:T(8,128)(2,1)S(1)}, u32[]{:S(2)}, u32[]{:S(2)}) collective-permute-start(bf16[8,256,128]{2,1,0:T(8,128)(2,1)S(1)} %pad_maximum_fusion), channel_id=1, source_target_pairs={{0,192},{1,193},{2,194},{3,195},{4,196},{5,197},{6,198},{7,199},{8... | collective-permute-start | bytes 1572872 | tf_op jit(solution)/shard_map/ppermute | solution.py:38
  242.6 18.8 %collective-permute-start.23 = (bf16[16,256,128]{2,1,0:T(8,128)(2,1)}, bf16[16,256,128]{2,1,0:T(8,128)(2,1)S(1)}, u32[]{:S(2)}, u32[]{:S(2)}) collective-permute-start(bf16[16,256,128]{2,1,0:T(8,128)(2,1)} %get-tuple-element.26), channel_id=1, source_target_pairs={{0,32},{1,33},{2,34},{3,35},{4,36},{5,37},{6,38},{7,39},{8,40},{9,... | collective-permute-start | bytes 3145736 | tf_op jit(solution)/shard_map/ppermute | solution.py:38
  255.1 7.4 %collective-permute-start.17 = (bf16[128,512]{1,0:T(8,128)(2,1)S(1)}, bf16[128,512]{1,0:T(8,128)(2,1)S(1)}, u32[]{:S(2)}, u32[]{:S(2)}) collective-permute-start(bf16[128,512]{1,0:T(8,128)(2,1)S(1)} %pad_maximum_fusion.3), channel_id=1, source_target_pairs={{0,32},{1,33},{2,34},{3,35},{4,36},{5,37},{6,38},{7,39},{8,40},{9,... | collective-permute-start | bytes 393224 | tf_op jit(solution)/shard_map/ppermute | solution.py:38
  255.9 1.3 copy-start.1
  260.9 1.7 collective-permute-start.18
  (3 other events, 2.0 us)

commit v2 on v1

--- a/solution.py
+++ b/solution.py
@@ -60,16 +60,11 @@
 
 def spread_kv(kv):
     kv = kv[None]
-    steps = (
-        lambda x, c, zh: (x, c, zh ^ 1),
-        lambda x, c, zh: (x, c, zh ^ 3),
-        lambda x, c, zh: (x ^ 1, c, zh),
-        lambda x, c, zh: (x ^ 3, c, zh),
-        other_core,
-    )
-    for rule in steps:
-        kv = jnp.concatenate([kv, send(kv, rule)])
-    return kv
+    for step in (1, 3):
+        kv = jnp.concatenate([kv, send(kv, lambda x, c, zh, step=step: (x, c, zh ^ step))])
+    near = send(kv, lambda x, c, zh: (x ^ 1, c, zh))
+    back = send(kv, lambda x, c, zh: (x ^ 3, c, zh))
+    return kv, near, back, send(near, lambda x, c, zh: (x ^ 3, c, zh))
 
 
 def vmem(count):
@@ -101,62 +96,75 @@
     )(wq, wk, gain)
 
 
+def small(size):
+    return pltpu.CompilerParams(vmem_limit_bytes=size << 20)
+
+
 def project_kernel(count, at, *refs):
-    parts, (wa, wb, wk), outs = refs[: 4 * count], refs[4 * count : 4 * count + 3], refs[4 * count + 3 : -6]
-    rows, a_held, b_held, k_held, row_sems, w_sems = refs[-6:]
+    parts, (wa, wb), outs = refs[: 4 * count], refs[4 * count : 4 * count + 2], refs[4 * count + 2 : -7]
+    rows, a_held, b_held, ka_held, kb_held, row_sems, w_sems = refs[-7:]
     q_out, kv_out = outs[0], outs[-1]
     width = a_held.shape[1]
     base = 2 * width if len(outs) == 1 else 0
     a_copy = pltpu.make_async_copy(wa.at[:, :width], a_held, w_sems.at[0])
-    b_copy = pltpu.make_async_copy(wb.at[:, :width], b_held, w_sems.at[1])
-    k_copy = pltpu.make_async_copy(wk, k_held, w_sems.at[2])
-    a_copy.start()
+    later = [
+        pltpu.make_async_copy(wb.at[:, :width], b_held, w_sems.at[1]),
+        pltpu.make_async_copy(wa.at[:, width:], ka_held, w_sems.at[2]),
+        pltpu.make_async_copy(wb.at[:, width:], kb_held, w_sems.at[3]),
+    ]
     row_copies = []
     for p in range(count):
         for i in range(4):
-            for core in range(2):
-                there = (at[i] * 2 + core) * 64 * count + p * 64
-                there = rows.at[pl.ds(pl.multiple_of(there, 64), 64), :]
-                here = parts[p * 4 + i].at[core * 64 : (core + 1) * 64, :]
-                row_copies.append(pltpu.make_async_copy(here, there, row_sems.at[len(row_copies)]))
-    for copy in row_copies:
+            there = rows.at[p, pl.ds(pl.multiple_of(at[i] * 128, 128), 128), :]
+            row_copies.append(pltpu.make_async_copy(parts[p * 4 + i], there, row_sems.at[len(row_copies)]))
+    a_copy.start()
+    for copy in row_copies[:4]:
         copy.start()
     a_copy.wait()
-    for copy in row_copies:
+    for copy in row_copies[:4]:
         copy.wait()
-    b_copy.start()
-    k_copy.start()
+    for copy in row_copies[4:] + later:
+        copy.start()
     size = 256
 
-    def first(i, carry):
-        there = pl.ds(pl.multiple_of(i * size, size), size)
-        q_out[there, :width] = jnp.dot(rows[there, :], a_held[...], preferred_element_type=F32).astype(BF16)
-        for part in range(0, size, 128):
-            there = pl.ds(pl.multiple_of(i * size + part, 128), 128)
-            squares = jnp.zeros((128, 128), F32)
-            for k in range(0, rows.shape[1], 128):
-                v = rows[there, k : k + 128].astype(F32)
-                squares = squares + v * v
-            sums = jnp.broadcast_to(jnp.sum(squares, axis=1, keepdims=True), (128, 128))
-            high = sums.astype(BF16).astype(F32)
-            lane = lax.broadcasted_iota(jnp.int32, (128, 128), 1)
-            kv_out[there, base + 128 : base + 256] = jnp.where(lane < 64, high, sums - high).astype(BF16)
+    def store(out, p, i, lanes, got):
+        for k in range(size // 64):
+            there = pl.ds(pl.multiple_of((i * (size // 64) + k) * 64 * count + p * 64, 64), 64)
+            out[there, lanes] = got[k * 64 : (k + 1) * 64]
+
+    def first(p, i, carry):
+        here = pl.ds(pl.multiple_of(i * size, size), size)
+        got = jnp.dot(rows[p, here, :], a_held[...], preferred_element_type=F32).astype(BF16)
+        store(q_out, p, i, slice(0, width), got)
+        squares = jnp.zeros((size, 128), F32)
+        for k in range(0, rows.shape[2], 128):
+            v = rows[p, here, k : k + 128].astype(F32)
+            squares = squares + v * v
+        sums = jnp.broadcast_to(jnp.sum(squares, axis=1, keepdims=True), (size, 128))
+        high = sums.astype(BF16).astype(F32)
+        lane = lax.broadcasted_iota(jnp.int32, (size, 128), 1)
+        store(kv_out, p, i, slice(base + 128, base + 256), jnp.where(lane < 64, high, sums - high).astype(BF16))
         return carry
 
-    def second(i, carry):
-        there = pl.ds(pl.multiple_of(i * size, size), size)
-        kv_out[there, base : base + 128] = jnp.dot(
-            rows[there, :], k_held[...], preferred_element_type=F32
-        ).astype(BF16)
-        q_out[there, width : 2 * width] = jnp.dot(
-            rows[there, :], b_held[...], preferred_element_type=F32
-        ).astype(BF16)
+    def second(p, i, carry):
+        here = pl.ds(pl.multiple_of(i * size, size), size)
+        got = jnp.dot(rows[p, here, :], b_held[...], preferred_element_type=F32).astype(BF16)
+        store(q_out, p, i, slice(width, 2 * width), got)
+        got = jnp.dot(rows[p, here, :], ka_held[...], preferred_element_type=F32).astype(BF16)
+        store(kv_out, p, i, slice(base, base + 128), got)
         return carry
 
-    lax.fori_loop(0, rows.shape[0] // size, first, 0)
-    b_copy.wait()
-    k_copy.wait()
-    lax.fori_loop(0, rows.shape[0] // size, second, 0)
+    for p in range(count):
+        if p:
+            for copy in row_copies[4 * p : 4 * p + 4]:
+                copy.wait()
+        lax.fori_loop(0, 512 // size, functools.partial(first, p), 0)
+    for copy in later:
+        copy.wait()
+    lane = lax.broadcasted_iota(jnp.int32, ka_held.shape, 1)
+    ka_held[...] = jnp.where(lane // 64 == at[4], ka_held[...].astype(F32), kb_held[...].astype(F32)).astype(BF16)
+    for p in range(count):
+        lax.fori_loop(0, 512 // size, functools.partial(second, p), 0)
 
 
 def project(at, parts, weights, split):
@@ -166,15 +174,16 @@
     return pl.pallas_call(
         functools.partial(project_kernel, count),
         out_shape=tuple(jax.ShapeDtypeStruct((512 * count, v), BF16) for v in widths),
-        in_specs=[smem()] + [pl.BlockSpec(memory_space=pl.ANY)] * (4 * count + 3),
+        in_specs=[smem()] + [pl.BlockSpec(memory_space=pl.ANY)] * (4 * count + 2),
         out_specs=tuple(vmem(len(widths))),
         scratch_shapes=[
-            pltpu.VMEM((512 * count, depth), BF16),
+            pltpu.VMEM((count, 512, depth), BF16),
             pltpu.VMEM((depth, width), BF16),
             pltpu.VMEM((depth, width), BF16),
             pltpu.VMEM((depth, 128), BF16),
-            pltpu.SemaphoreType.DMA((8 * count,)),
-            pltpu.SemaphoreType.DMA((3,)),
+            pltpu.VMEM((depth, 128), BF16),
+            pltpu.SemaphoreType.DMA((4 * count,)),
+            pltpu.SemaphoreType.DMA((4,)),
         ],
         cost_estimate=pl.CostEstimate(
             flops=2 * 512 * count * depth * 1152, bytes_accessed=(5 + 3 * count) << 20, transcendentals=0
@@ -253,33 +262,54 @@
             out_specs=tuple(pl.BlockSpec((block, v), lambda n, at: (0, 0)) for v in widths),
         ),
         cost_estimate=pl.CostEstimate(flops=1 << 20, bytes_accessed=2 << 20, transcendentals=0),
+        compiler_params=small(24),
     )(rows, *came, *[v for v in tables for _ in parts])
 
 
-def last_kernel(at, pick, q_near, q_far, q_near_came, q_far_came, kv, q_out, kv_out):
+def owned_kernel(pick, own, near, back, far, out):
     lane = lax.broadcasted_iota(jnp.int32, (64, 128), 1)
+    for s in range(2):
+        x_off, odd = pick[4 + 2 * s], pick[5 + 2 * s]
+
+        def part(g, t, x_off=x_off):
+            rows = slice(BACK[(t - g) % 4] * 64, BACK[(t - g) % 4] * 64 + 64)
+            got = [v[pick[g], rows, :].astype(F32) for v in (own, near, far, back)]
+            low = jnp.where(x_off == 0, got[0], got[1])
+            return jnp.where(x_off < 2, low, jnp.where(x_off == 2, got[2], got[3]))
+
+        for t in range(4):
+            for half in range(2):
+                a, b = part(2 * half, t), part(2 * half + 1, t)
+                low = jnp.where(odd == 0, a, pltpu.roll(a, 64, 1))
+                high = jnp.where(odd == 0, pltpu.roll(b, 64, 1), b)
+                out[s, t * 64 : (t + 1) * 64, half * 128 : (half + 1) * 128] = jnp.where(lane < 64, low, high).astype(BF16)
+
+
+def owned(pick, arrays):
+    return pl.pallas_call(
+        owned_kernel,
+        out_shape=jax.ShapeDtypeStruct((2, 256, 256), BF16),
+        in_specs=[smem()] + vmem(4),
+        out_specs=vmem(1)[0],
+        cost_estimate=pl.CostEstimate(flops=1 << 20, bytes_accessed=1 << 20, transcendentals=0),
+        compiler_params=small(24),
+        name="owned",
+    )(pick, *arrays)
+
+
+def last_kernel(at, pick, q_near, q_far, q_near_came, q_far_came, kv, kv_came, q_out, kv_out):
     for p in range(4):
         here = slice(p % 2 * 64, p % 2 * 64 + 64)
         rows = pl.ds(pl.multiple_of(at[p] * 64, 64), 64)
         q_out[rows, :] = (q_near, q_far)[p // 2][here, :]
         rows = pl.ds(pl.multiple_of(at[4 + p] * 64, 64), 64)
         q_out[rows, :] = (q_near_came, q_far_came)[p // 2][here, :]
+    core = pick[8]
     for s in range(2):
-        x_off, odd = pick[4 + 2 * s], pick[5 + 2 * s]
         for t in range(4):
-            for core in range(2):
-
-                def part(g, t=t, core=core, x_off=x_off):
-                    i = BACK[(t - g) % 4]
-                    return kv[pick[8 + core] + x_off + pick[g], i * 64 : (i + 1) * 64, :].astype(F32)
-
-                for half in range(2):
-                    a, b = part(2 * half), part(2 * half + 1)
-                    low = jnp.where(odd == 0, a, pltpu.roll(a, 64, 1))
-                    high = jnp.where(odd == 0, pltpu.roll(b, 64, 1), b)
-                    kv_out[s, t * 128 + core * 64 : t * 128 + core * 64 + 64, half * 128 : (half + 1) * 128] = jnp.where(
-                        lane < 64, low, high
-                    ).astype(BF16)
+            here = slice(t * 64, (t + 1) * 64)
+            kv_out[s, pl.ds(pl.multiple_of(t * 128 + core * 64, 64), 64), :] = kv[s, here, :]
+            kv_out[s, pl.ds(pl.multiple_of(t * 128 + (1 - core) * 64, 64), 64), :] = kv_came[s, here, :]
 
 
 def last(at, pick, arrays, tokens):
@@ -292,6 +322,7 @@
         in_specs=[smem(), smem()] + vmem(len(arrays)),
         out_specs=tuple(vmem(2)),
         cost_estimate=pl.CostEstimate(flops=1 << 10, bytes_accessed=4 << 20, transcendentals=0),
+        compiler_params=small(24),
         name="last",
     )(at, pick, *arrays)
 
@@ -316,7 +347,7 @@
     mine_w = prepare(w_query, w_keyval, gain)
     other_w = send(mine_w, other_core)
     lane = lax.broadcasted_iota(jnp.int32, (1, 128), 1)
-    weights = (mine_w, other_w, jnp.where(lane // 64 == core, mine_w[:, width:], other_w[:, width:]))
+    weights = (mine_w, other_w)
 
     def tables(column, is_key):
         inv_freq = jnp.exp((column // 2).astype(F32) * (-2.0 * math.log(ROPE_BASE) / HD))
@@ -327,13 +358,13 @@
     all_tables = (*tables(lane, True), *tables((gy % 2) * 64 + lane % 64, gy < 2))
 
     ring = jnp.array([0, 3, 1, 2], jnp.int32)
-    place = (x + ring) % 4
+    place = jnp.concatenate([(x + ring) % 4, core[None]])
     source_z = (gy + ring) % 4
     at = jnp.concatenate([source_z * 2 + core, source_z * 2 + 1 - core])
     wanted = lax.dynamic_slice_in_dim(keyval_order, gy * 2, 2, 0)
-    four, two = jnp.arange(4, dtype=jnp.int32), jnp.arange(2, dtype=jnp.int32)
+    four = jnp.arange(4, dtype=jnp.int32)
     pick = jnp.concatenate(
-        [gray(four ^ gy), jnp.stack([gray(wanted // 2 ^ x) * 4, wanted % 2], axis=1).reshape(4), (two ^ core) * 16]
+        [gray(four ^ gy), jnp.stack([wanted // 2 ^ x, wanted % 2], axis=1).reshape(4), core[None]]
     )
 
     left, right = send(mine, along_z(1)), send(mine, along_z(-1))
@@ -358,8 +389,10 @@
     q_near = jnp.concatenate(q_own[:2])
     q_near_came = send(jnp.concatenate(q_other[:2]), other_core)
     q_far_came = send(q_other[2], other_core)
-    kv = spread_kv(jnp.concatenate(kvs))
-    return last(at, pick, (q_near, q_own[2], q_near_came, q_far_came, kv), tokens)
+    kv_parts = spread_kv(jnp.concatenate(kvs))
+    kv = owned(pick, kv_parts)
+    kv_came = send(kv, other_core)
+    return last(at, pick, (q_near, q_own[2], q_near_came, q_far_came, kv, kv_came), tokens)
 
 
 def solution(mesh):

time: 268 us -> 260 us (0.970)
  starting transfers between devices: 71.9 us -> 80.3 us
  Pallas kernels: 47.2 us -> 39.8 us
  other arithmetic: 12.1 us -> 5.28 us
  local copies, waits for them, and re-layouts: 12.3 us -> 7.51 us
  waiting for transfers between devices: 105 us -> 108 us
    pallas_call x4, Pallas kernels: 12.3 us -> 3.52 us  [finish(): pl.pallas_call(functools.partial(kernel, len(parts)), out_shape=tuple((ja...]
    ppermute x24 -> x25, starting transfers between devices: 58.6 us -> 67 us  [send(): return lax.ppermute(value, AXES, moves(rule))]
    ppermute x24 -> x25, waiting for transfers between devices: 105 us -> 108 us  [send(): return lax.ppermute(value, AXES, moves(rule))]
    unnamed x52 -> x49, local copies, waits for them, and re-layouts: 7.74 us -> 5.88 us
  transfers between devices with their start and end apart: 27 -> 28, of which waited for: 17 -> 17; matrix products, arithmetic and copies ran while one was open for 6% -> 2% of each run, Pallas kernels for 15% -> 13%
where the time goes in v2:
time: 260 us; the launch traced here: 259 us
  waiting for transfers between devices  108 us (42%)
  starting transfers between devices  80.3 us (31%)
  Pallas kernels  39.8 us (15%)
  blocking collectives  17.2 us (7%)
  local copies, waits for them, and re-layouts  7.51 us (3%)
  other arithmetic  5.28 us (2%)
    ppermute x25, waiting for transfers between devices, send(): return lax.ppermute(value, AXES, moves(rule))  108 us
    ppermute x25, starting transfers between devices, send(): return lax.ppermute(value, AXES, moves(rule))  67 us
    pallas_call x3, Pallas kernels, project(): pl.pallas_call(functools.partial(project_kernel, count), out_shape=tuple(...  28.3 us
    all_to_all x1, blocking collectives, exchange(): return lax.all_to_all(value, axis, 0, 0, tiled=True)  17.2 us
    all_to_all x3, starting transfers between devices, exchange(): return lax.all_to_all(value, axis, 0, 0, tiled=True)  13.3 us
    unnamed x49, local copies, waits for them, and re-layouts  5.88 us
  transfers between devices with their start and end apart: 28, of which 17 were waited for; matrix products, arithmetic and copies ran while one was open for 2% of the time, Pallas kernels for 13%

profile of v2, /device:TPU:1, one launch (start us, length us, event | category | flops | bytes accessed | tf_op | source)
XLA Modules:
  0.0 259.0 jit_solution(17084816384662581441)
XLA Ops:
  1.3 1.4 copy.13.gain
  2.7 2.0 copy.12.wk
  4.7 4.4 %prepare.1.refs_4_.refs_8_ = bf16[2048,640]{1,0:T(8,128)(2,1)} custom-call(bf16[2048,512]{1,0:T(8,128)(2,1)} %wq.1, bf16[2048,64]{1,0:T(8,128)(2,1)} %copy.12.wk, f32[2048,1]{1,0:T(8,128)} %copy.13.gain), custom_call_target="tpu_custom_call" | custom-call | flops 1048576 | bytes 5242880 | tf_op jit(solution)/shard_map/prepare/pallas_call | solution.py:89
  9.1 3.2 %collective-permute-start.4 = (bf16[2048,640]{1,0:T(8,128)(2,1)}, bf16[2048,640]{1,0:T(8,128)(2,1)}, u32[]{:S(2)}, u32[]{:S(2)}) collective-permute-start(bf16[2048,640]{1,0:T(8,128)(2,1)} %prepare.1.refs_4_.refs_8_), channel_id=1, source_target_pairs={{0,32},{1,33},{2,34},{3,35},{4,36},{5,37},{6,38},{7,39},{8,40},{9,... | collective-permute-start | bytes 7864328 | tf_op jit(solution)/shard_map/ppermute | solution.py:38
  12.5 5.0 %collective-permute-done = bf16[64,2048]{1,0:T(8,128)(2,1)S(1)} collective-permute-done((bf16[64,2048]{1,0:T(8,128)(2,1)S(1)}, bf16[64,2048]{1,0:T(8,128)(2,1)S(1)}, u32[]{:S(2)}, u32[]{:S(2)}) %collective-permute-start) | collective-permute-done | bytes 262176 | tf_op jit(solution)/shard_map/ppermute | solution.py:38
  17.5 1.4 collective-permute-start.5
  18.9 3.1 %collective-permute-start.9 = (bf16[128,2048]{1,0:T(8,128)(2,1)S(1)}, bf16[128,2048]{1,0:T(8,128)(2,1)S(1)}, u32[]{:S(2)}, u32[]{:S(2)}) collective-permute-start(bf16[128,2048]{1,0:T(8,128)(2,1)S(1)} %maximum_select_fusion.refs_0_), channel_id=1, source_target_pairs={{0,24},{1,25},{2,26},{3,27},{4,28},{5,29},{6,30},{7,31},{8,0},{9,1... | collective-permute-start | bytes 1572872 | tf_op jit(solution)/shard_map/ppermute | solution.py:38
  22.0 16.2 %collective-permute-done.5.refs_0_ = bf16[128,2048]{1,0:T(8,128)(2,1)S(1)} collective-permute-done((bf16[128,2048]{1,0:T(8,128)(2,1)S(1)}, bf16[128,2048]{1,0:T(8,128)(2,1)S(1)}, u32[]{:S(2)}, u32[]{:S(2)}) %collective-permute-start.5) | collective-permute-done | bytes 524320 | tf_op jit(solution)/shard_map/ppermute | solution.py:38
  38.2 7.3 %collective-permute-start.13 = (bf16[128,2048]{1,0:T(8,128)(2,1)S(1)}, bf16[128,2048]{1,0:T(8,128)(2,1)S(1)}, u32[]{:S(2)}, u32[]{:S(2)}) collective-permute-start(bf16[128,2048]{1,0:T(8,128)(2,1)S(1)} %collective-permute-done.5.refs_0_), channel_id=1, source_target_pairs={{0,8},{1,9},{2,10},{3,11},{4,12},{5,13},{6,14},{7,15},{8,16},{9,17... | collective-permute-start | bytes 1572872 | tf_op jit(solution)/shard_map/ppermute | solution.py:38
  46.3 1.2 collective-permute-start.10
  47.5 19.7 %collective-permute-done.13.refs_4_ = bf16[128,2048]{1,0:T(8,128)(2,1)S(1)} collective-permute-done((bf16[128,2048]{1,0:T(8,128)(2,1)S(1)}, bf16[128,2048]{1,0:T(8,128)(2,1)S(1)}, u32[]{:S(2)}, u32[]{:S(2)}) %collective-permute-start.13) | collective-permute-done | bytes 524320 | tf_op jit(solution)/shard_map/ppermute | solution.py:38
  67.2 2.5 collective-permute-start.15
  70.2 0.9 collective-permute-start.14
  71.2 7.0 %collective-permute-done.15.refs_6_ = bf16[128,2048]{1,0:T(8,128)(2,1)} collective-permute-done((bf16[128,2048]{1,0:T(8,128)(2,1)S(1)}, bf16[128,2048]{1,0:T(8,128)(2,1)}, u32[]{:S(2)}, u32[]{:S(2)}) %collective-permute-start.15) | collective-permute-done | bytes 524320 | tf_op jit(solution)/shard_map/ppermute | solution.py:38
  78.2 3.5 %collective-permute-start.16 = (bf16[128,2048]{1,0:T(8,128)(2,1)}, bf16[128,2048]{1,0:T(8,128)(2,1)}, u32[]{:S(2)}, u32[]{:S(2)}) collective-permute-start(bf16[128,2048]{1,0:T(8,128)(2,1)} %collective-permute-done.15.refs_6_), channel_id=1, source_target_pairs={{0,192},{1,193},{2,194},{3,195},{4,196},{5,197},{6,198},{7,199},{8... | collective-permute-start | bytes 1572872 | tf_op jit(solution)/shard_map/ppermute | solution.py:38
  82.3 7.1 %collective-permute-done.11.refs_2_ = bf16[128,2048]{1,0:T(8,128)(2,1)} collective-permute-done((bf16[128,2048]{1,0:T(8,128)(2,1)S(1)}, bf16[128,2048]{1,0:T(8,128)(2,1)}, u32[]{:S(2)}, u32[]{:S(2)}) %collective-permute-start.11) | collective-permute-done | bytes 524320 | tf_op jit(solution)/shard_map/ppermute | solution.py:38
  89.5 1.0 collective-permute-start.1
  90.5 2.5 collective-permute-done.12.refs_3_
  93.0 7.8 %collective-permute-done.16.refs_7_ = bf16[128,2048]{1,0:T(8,128)(2,1)} collective-permute-done((bf16[128,2048]{1,0:T(8,128)(2,1)}, bf16[128,2048]{1,0:T(8,128)(2,1)}, u32[]{:S(2)}, u32[]{:S(2)}) %collective-permute-start.16) | collective-permute-done | bytes 524320 | tf_op jit(solution)/shard_map/ppermute | solution.py:38
  100.8 12.5 %shard_map.90 = (bf16[1024,1024]{1,0:T(8,128)(2,1)}, bf16[1024,256]{1,0:T(8,128)(2,1)}) custom-call(s32[5]{0:T(128)} %pad_add_fusion.3.at, bf16[128,2048]{1,0:T(8,128)(2,1)} %copy-done.17, bf16[128,2048]{1,0:T(8,128)(2,1)} %copy-done.19, bf16[128,2048]{1,0:T(8,128)(2,1)} %collective-permute-done.11.refs_2_, ...), custom_call_target="tpu_custom_call" | custom-call | flops 4831838208 | bytes 11534336 | tf_op jit(solution)/shard_map/pallas_call | solution.py:174
  113.4 4.6 %all-to-all-start.3 = ((bf16[8,128,256]{2,1,0:T(8,128)(2,1)}), bf16[8,128,256]{2,1,0:T(8,128)(2,1)S(1)}, u32[]{:S(2)}, u32[]{:S(2)}) async-start(bf16[8,128,256]{2,1,0:T(8,128)(2,1)} %bitcast.15), calls=%async_computation.3 | async-start | bytes 1048576 | tf_op jit(solution)/shard_map/all_to_all | solution.py:54
  117.9 3.5 %collective-permute-start.2 = (bf16[128,2048]{1,0:T(8,128)(2,1)S(1)}, bf16[128,2048]{1,0:T(8,128)(2,1)S(1)}, u32[]{:S(2)}, u32[]{:S(2)}) collective-permute-start(bf16[128,2048]{1,0:T(8,128)(2,1)S(1)} %maximum_select_fusion.refs_0_), channel_id=1, source_target_pairs={{0,192},{1,193},{2,194},{3,195},{4,196},{5,197},{6,198},{7,199},{8... | collective-permute-start | bytes 1572872 | tf_op jit(solution)/shard_map/ppermute | solution.py:38
  121.4 7.8 %collective-permute-done.2.refs_2_ = bf16[128,2048]{1,0:T(8,128)(2,1)S(1)} collective-permute-done((bf16[128,2048]{1,0:T(8,128)(2,1)S(1)}, bf16[128,2048]{1,0:T(8,128)(2,1)S(1)}, u32[]{:S(2)}, u32[]{:S(2)}) %collective-permute-start.2) | collective-permute-done | bytes 524320 | tf_op jit(solution)/shard_map/ppermute | solution.py:38
  129.3 3.3 %collective-permute-done.3.refs_3_ = bf16[128,2048]{1,0:T(8,128)(2,1)S(1)} collective-permute-done((bf16[128,2048]{1,0:T(8,128)(2,1)}, bf16[128,2048]{1,0:T(8,128)(2,1)S(1)}, u32[]{:S(2)}, u32[]{:S(2)}) %collective-permute-start.3) | collective-permute-done | bytes 524320 | tf_op jit(solution)/shard_map/ppermute | solution.py:38
  133.4 7.9 %shard_map.86 = bf16[512,1280]{1,0:T(8,128)(2,1)} custom-call(s32[5]{0:T(128)} %pad_add_fusion.3.at, bf16[128,2048]{1,0:T(8,128)(2,1)} %copy-done.11, bf16[128,2048]{1,0:T(8,128)(2,1)} %collective-permute-done.1.refs_1_, bf16[128,2048]{1,0:T(8,128)(2,1)} %copy-done.22, bf16[128,2048]{1,0:T(8,128)(2,1)} %copy-done.23, ...), custom_call_target="tpu_custom_call" | custom-call | flops 2415919104 | bytes 8388608 | tf_op jit(solution)/shard_map/pallas_call | solution.py:174
  141.3 4.8 %all-to-all-start = ((bf16[8,64,1280]{2,1,0:T(8,128)(2,1)}), bf16[8,64,1280]{2,1,0:T(8,128)(2,1)S(1)}, u32[]{:S(2)}, u32[]{:S(2)}) async-start(bf16[8,64,1280]{2,1,0:T(8,128)(2,1)} %bitcast.13), calls=%async_computation | async-start | bytes 2621440 | tf_op jit(solution)/shard_map/all_to_all | solution.py:54
  147.6 6.6 %collective-permute-done.7.refs_2_ = bf16[128,2048]{1,0:T(8,128)(2,1)S(1)} collective-permute-done((bf16[128,2048]{1,0:T(8,128)(2,1)S(1)}, bf16[128,2048]{1,0:T(8,128)(2,1)S(1)}, u32[]{:S(2)}, u32[]{:S(2)}) %collective-permute-start.7) | collective-permute-done | bytes 524320 | tf_op jit(solution)/shard_map/ppermute | solution.py:38
  154.1 2.6 %collective-permute-start.8 = (bf16[128,2048]{1,0:T(8,128)(2,1)S(1)}, bf16[128,2048]{1,0:T(8,128)(2,1)}, u32[]{:S(2)}, u32[]{:S(2)}) collective-permute-start(bf16[128,2048]{1,0:T(8,128)(2,1)S(1)} %collective-permute-done.7.refs_2_), channel_id=1, source_target_pairs={{0,192},{1,193},{2,194},{3,195},{4,196},{5,197},{6,198},{7,199},{8... | collective-permute-start | bytes 1572872 | tf_op jit(solution)/shard_map/ppermute | solution.py:38
  157.6 7.9 %collective-permute-done.8.refs_3_ = bf16[128,2048]{1,0:T(8,128)(2,1)} collective-permute-done((bf16[128,2048]{1,0:T(8,128)(2,1)S(1)}, bf16[128,2048]{1,0:T(8,128)(2,1)}, u32[]{:S(2)}, u32[]{:S(2)}) %collective-permute-start.8) | collective-permute-done | bytes 524320 | tf_op jit(solution)/shard_map/ppermute | solution.py:38
  165.5 7.9 %shard_map.88 = bf16[512,1280]{1,0:T(8,128)(2,1)} custom-call(s32[5]{0:T(128)} %pad_add_fusion.3.at, bf16[128,2048]{1,0:T(8,128)(2,1)} %copy-done.16, bf16[128,2048]{1,0:T(8,128)(2,1)} %copy-done.21, bf16[128,2048]{1,0:T(8,128)(2,1)} %copy-done.20, bf16[128,2048]{1,0:T(8,128)(2,1)} %collective-permute-done.8.refs_3_, ...), custom_call_target="tpu_custom_call" | custom-call | flops 2415919104 | bytes 8388608 | tf_op jit(solution)/shard_map/pallas_call | solution.py:174
  173.4 17.2 %all_to_all.20.came = bf16[8,64,1280]{2,1,0:T(8,128)(2,1)} all-to-all(bf16[8,64,1280]{2,1,0:T(8,128)(2,1)} %bitcast.14), channel_id=1, replica_groups=mesh['gx'=8,'gy'=4,'gz'=8] {'gz'}, dimensions={0} | all-to-all | bytes 2621440 | tf_op jit(solution)/shard_map/all_to_all | solution.py:54
  190.7 4.0 %all-to-all-start.2 = ((bf16[8,128,1024]{2,1,0:T(8,128)(2,1)}), bf16[8,128,1024]{2,1,0:T(8,128)(2,1)S(1)}, u32[]{:S(2)}, u32[]{:S(2)}) async-start(bf16[8,128,1024]{2,1,0:T(8,128)(2,1)} %bitcast.12), calls=%async_computation.2 | async-start | bytes 4194304 | tf_op jit(solution)/shard_map/all_to_all | solution.py:54
  194.8 1.9 fusion.3
  199.2 5.6 %collective-permute-start.19 = (bf16[1,256,128]{2,1,0:T(8,128)(2,1)S(1)}, bf16[1,256,128]{2,1,0:T(8,128)(2,1)S(1)}, u32[]{:S(2)}, u32[]{:S(2)}) collective-permute-start(bf16[1,256,128]{2,1,0:T(8,128)(2,1)S(1)} %maximum_bitcast_fusion), channel_id=1, source_target_pairs={{0,8},{1,9},{2,10},{3,11},{4,12},{5,13},{6,14},{7,15},{8,0},{9,1},... | collective-permute-start | bytes 196616 | tf_op jit(solution)/shard_map/ppermute | solution.py:38
  204.8 6.1 %collective-permute-done.19 = bf16[1,256,128]{2,1,0:T(8,128)(2,1)S(1)} collective-permute-done((bf16[1,256,128]{2,1,0:T(8,128)(2,1)S(1)}, bf16[1,256,128]{2,1,0:T(8,128)(2,1)S(1)}, u32[]{:S(2)}, u32[]{:S(2)}) %collective-permute-start.19) | collective-permute-done | bytes 65568 | tf_op jit(solution)/shard_map/ppermute | solution.py:38
  211.6 10.7 %collective-permute-start.20 = (bf16[2,256,128]{2,1,0:T(8,128)(2,1)S(1)}, bf16[2,256,128]{2,1,0:T(8,128)(2,1)}, u32[]{:S(2)}, u32[]{:S(2)}) collective-permute-start(bf16[2,256,128]{2,1,0:T(8,128)(2,1)S(1)} %pad_maximum_fusion.3), channel_id=1, source_target_pairs={{0,24},{1,25},{2,26},{3,27},{4,28},{5,29},{6,30},{7,31},{8,16},{9,... | collective-permute-start | bytes 393224 | tf_op jit(solution)/shard_map/ppermute | solution.py:38
  222.2 3.9 %collective-permute-done.20 = bf16[2,256,128]{2,1,0:T(8,128)(2,1)} collective-permute-done((bf16[2,256,128]{2,1,0:T(8,128)(2,1)S(1)}, bf16[2,256,128]{2,1,0:T(8,128)(2,1)}, u32[]{:S(2)}, u32[]{:S(2)}) %collective-permute-start.20) | collective-permute-done | bytes 131104 | tf_op jit(solution)/shard_map/ppermute | solution.py:38
  226.1 1.0 pad_maximum_fusion.own
  227.3 3.0 %collective-permute-start.22 = (bf16[4,256,128]{2,1,0:T(8,128)(2,1)S(1)}, bf16[4,256,128]{2,1,0:T(8,128)(2,1)}, u32[]{:S(2)}, u32[]{:S(2)}) collective-permute-start(bf16[4,256,128]{2,1,0:T(8,128)(2,1)S(1)} %pad_maximum_fusion.own), channel_id=1, source_target_pairs={{0,192},{1,193},{2,194},{3,195},{4,196},{5,197},{6,198},{7,199},{8... | collective-permute-start | bytes 786440 | tf_op jit(solution)/shard_map/ppermute | solution.py:38
  231.0 1.5 collective-permute-done.21.near
  232.5 2.9 %collective-permute-start.23 = (bf16[4,256,128]{2,1,0:T(8,128)(2,1)}, bf16[4,256,128]{2,1,0:T(8,128)(2,1)}, u32[]{:S(2)}, u32[]{:S(2)}) collective-permute-start(bf16[4,256,128]{2,1,0:T(8,128)(2,1)} %collective-permute-done.21.near), channel_id=1, source_target_pairs={{0,192},{1,193},{2,194},{3,195},{4,196},{5,197},{6,198},{7,199},{8... | collective-permute-start | bytes 786440 | tf_op jit(solution)/shard_map/ppermute | solution.py:38
  235.7 3.8 %collective-permute-done.23.far = bf16[4,256,128]{2,1,0:T(8,128)(2,1)} collective-permute-done((bf16[4,256,128]{2,1,0:T(8,128)(2,1)}, bf16[4,256,128]{2,1,0:T(8,128)(2,1)}, u32[]{:S(2)}, u32[]{:S(2)}) %collective-permute-start.23) | collective-permute-done | bytes 262176 | tf_op jit(solution)/shard_map/ppermute | solution.py:38
  239.5 0.9 copy-done.4
  240.4 1.5 owned.1.kv
  241.9 11.7 %collective-permute-start.24 = (bf16[2,256,256]{2,1,0:T(8,128)(2,1)S(1)}, bf16[2,256,256]{2,1,0:T(8,128)(2,1)}, u32[]{:S(2)}, u32[]{:S(2)}) collective-permute-start(bf16[2,256,256]{2,1,0:T(8,128)(2,1)S(1)} %owned.1.kv), channel_id=1, source_target_pairs={{0,32},{1,33},{2,34},{3,35},{4,36},{5,37},{6,38},{7,39},{8,40},{9,... | collective-permute-start | bytes 786440 | tf_op jit(solution)/shard_map/ppermute | solution.py:38
  254.3 1.1 shard_map.91
  256.1 0.9 collective-permute-done.18.q_far_came
  257.0 2.0 last.1
  (92 shorter events, 11.6 us)
Async XLA Ops:
  4.7 7.6 %copy-start.10 = (bf16[128,2048]{1,0:T(8,128)(2,1)S(1)}, bf16[128,2048]{1,0:T(8,128)(2,1)}, u32[]{:S(2)}) copy-start(bf16[128,2048]{1,0:T(8,128)(2,1)} %param.7) | copy-start | bytes 1572868
  9.1 72.6 %copy-start.15 = (s32[4]{0:T(128)S(1)}, s32[4]{0:T(128)}, u32[]{:S(2)}) copy-start(s32[4]{0:T(128)} %constant.138.clone) | copy-start | bytes 52
  9.1 91.7 %collective-permute-start.4 = (bf16[2048,640]{1,0:T(8,128)(2,1)}, bf16[2048,640]{1,0:T(8,128)(2,1)}, u32[]{:S(2)}, u32[]{:S(2)}) collective-permute-start(bf16[2048,640]{1,0:T(8,128)(2,1)} %prepare.1.refs_4_.refs_8_), channel_id=1, source_target_pairs={{0,32},{1,33},{2,34},{3,35},{4,36},{5,37},{6,38},{7,39},{8,40},{9,... | collective-permute-start | bytes 7864328 | tf_op jit(solution)/shard_map/ppermute | solution.py:38
  12.3 5.1 %collective-permute-start = (bf16[64,2048]{1,0:T(8,128)(2,1)S(1)}, bf16[64,2048]{1,0:T(8,128)(2,1)S(1)}, u32[]{:S(2)}, u32[]{:S(2)}) collective-permute-start(bf16[64,2048]{1,0:T(8,128)(2,1)S(1)} %get-tuple-element.27), channel_id=1, source_target_pairs={{0,32},{1,33},{2,34},{3,35},{4,36},{5,37},{6,38},{7,39},{8,40},{9,... | collective-permute-start | bytes 786440 | tf_op jit(solution)/shard_map/ppermute | solution.py:38
  17.5 100.4 %copy-start.11 = (bf16[128,2048]{1,0:T(8,128)(2,1)}, bf16[128,2048]{1,0:T(8,128)(2,1)S(1)}, u32[]{:S(2)}) copy-start(bf16[128,2048]{1,0:T(8,128)(2,1)S(1)} %maximum_select_fusion.refs_0_) | copy-start | bytes 1572868
  17.5 20.7 %collective-permute-start.5 = (bf16[128,2048]{1,0:T(8,128)(2,1)S(1)}, bf16[128,2048]{1,0:T(8,128)(2,1)S(1)}, u32[]{:S(2)}, u32[]{:S(2)}) collective-permute-start(bf16[128,2048]{1,0:T(8,128)(2,1)S(1)} %maximum_select_fusion.refs_0_), channel_id=1, source_target_pairs={{0,8},{1,9},{2,10},{3,11},{4,12},{5,13},{6,14},{7,15},{8,16},{9,17... | collective-permute-start | bytes 1572872 | tf_op jit(solution)/shard_map/ppermute | solution.py:38
  18.9 27.4 %collective-permute-start.9 = (bf16[128,2048]{1,0:T(8,128)(2,1)S(1)}, bf16[128,2048]{1,0:T(8,128)(2,1)S(1)}, u32[]{:S(2)}, u32[]{:S(2)}) collective-permute-start(bf16[128,2048]{1,0:T(8,128)(2,1)S(1)} %maximum_select_fusion.refs_0_), channel_id=1, source_target_pairs={{0,24},{1,25},{2,26},{3,27},{4,28},{5,29},{6,30},{7,31},{8,0},{9,1... | collective-permute-start | bytes 1572872 | tf_op jit(solution)/shard_map/ppermute | solution.py:38
  38.2 108.7 %copy-start.16 = (bf16[128,2048]{1,0:T(8,128)(2,1)}, bf16[128,2048]{1,0:T(8,128)(2,1)S(1)}, u32[]{:S(2)}) copy-start(bf16[128,2048]{1,0:T(8,128)(2,1)S(1)} %collective-permute-done.5.refs_0_) | copy-start | bytes 1572868
  38.2 28.9 %collective-permute-start.13 = (bf16[128,2048]{1,0:T(8,128)(2,1)S(1)}, bf16[128,2048]{1,0:T(8,128)(2,1)S(1)}, u32[]{:S(2)}, u32[]{:S(2)}) collective-permute-start(bf16[128,2048]{1,0:T(8,128)(2,1)S(1)} %collective-permute-done.5.refs_0_), channel_id=1, source_target_pairs={{0,8},{1,9},{2,10},{3,11},{4,12},{5,13},{6,14},{7,15},{8,16},{9,17... | collective-permute-start | bytes 1572872 | tf_op jit(solution)/shard_map/ppermute | solution.py:38
  46.3 54.5 %copy-start.17 = (bf16[128,2048]{1,0:T(8,128)(2,1)}, bf16[128,2048]{1,0:T(8,128)(2,1)S(1)}, u32[]{:S(2)}) copy-start(bf16[128,2048]{1,0:T(8,128)(2,1)S(1)} %collective-permute-done.9.refs_0_) | copy-start | bytes 1572868
  46.3 24.8 %collective-permute-start.10 = (bf16[128,2048]{1,0:T(8,128)(2,1)S(1)}, bf16[128,2048]{1,0:T(8,128)(2,1)S(1)}, u32[]{:S(2)}, u32[]{:S(2)}) collective-permute-start(bf16[128,2048]{1,0:T(8,128)(2,1)S(1)} %collective-permute-done.9.refs_0_), channel_id=1, source_target_pairs={{0,64},{1,65},{2,66},{3,67},{4,68},{5,69},{6,70},{7,71},{8,72},{9,... | collective-permute-start | bytes 1572872 | tf_op jit(solution)/shard_map/ppermute | solution.py:38
  67.2 33.6 %copy-start.18 = (bf16[128,2048]{1,0:T(8,128)(2,1)}, bf16[128,2048]{1,0:T(8,128)(2,1)S(1)}, u32[]{:S(2)}) copy-start(bf16[128,2048]{1,0:T(8,128)(2,1)S(1)} %collective-permute-done.13.refs_4_) | copy-start | bytes 1572868
  67.2 11.1 %collective-permute-start.15 = (bf16[128,2048]{1,0:T(8,128)(2,1)S(1)}, bf16[128,2048]{1,0:T(8,128)(2,1)}, u32[]{:S(2)}, u32[]{:S(2)}) collective-permute-start(bf16[128,2048]{1,0:T(8,128)(2,1)S(1)} %collective-permute-done.13.refs_4_), channel_id=1, source_target_pairs={{0,192},{1,193},{2,194},{3,195},{4,196},{5,197},{6,198},{7,199},{8... | collective-permute-start | bytes 1572872 | tf_op jit(solution)/shard_map/ppermute | solution.py:38
  69.6 19.8 %collective-permute-start.11 = (bf16[128,2048]{1,0:T(8,128)(2,1)S(1)}, bf16[128,2048]{1,0:T(8,128)(2,1)}, u32[]{:S(2)}, u32[]{:S(2)}) collective-permute-start(bf16[128,2048]{1,0:T(8,128)(2,1)S(1)} %collective-permute-done.9.refs_0_), channel_id=1, source_target_pairs={{0,192},{1,193},{2,194},{3,195},{4,196},{5,197},{6,198},{7,199},{8... | collective-permute-start | bytes 1572872 | tf_op jit(solution)/shard_map/ppermute | solution.py:38
  70.2 22.8 %collective-permute-start.14 = (bf16[128,2048]{1,0:T(8,128)(2,1)S(1)}, bf16[128,2048]{1,0:T(8,128)(2,1)}, u32[]{:S(2)}, u32[]{:S(2)}) collective-permute-start(bf16[128,2048]{1,0:T(8,128)(2,1)S(1)} %collective-permute-done.13.refs_4_), channel_id=1, source_target_pairs={{0,64},{1,65},{2,66},{3,67},{4,68},{5,69},{6,70},{7,71},{8,72},{9,... | collective-permute-start | bytes 1572872 | tf_op jit(solution)/shard_map/ppermute | solution.py:38
  71.1 29.7 %copy-start.19 = (bf16[128,2048]{1,0:T(8,128)(2,1)}, bf16[128,2048]{1,0:T(8,128)(2,1)S(1)}, u32[]{:S(2)}) copy-start(bf16[128,2048]{1,0:T(8,128)(2,1)S(1)} %collective-permute-done.10.refs_1_) | copy-start | bytes 1572868
  71.1 21.8 %collective-permute-start.12 = (bf16[128,2048]{1,0:T(8,128)(2,1)S(1)}, bf16[128,2048]{1,0:T(8,128)(2,1)}, u32[]{:S(2)}, u32[]{:S(2)}) collective-permute-start(bf16[128,2048]{1,0:T(8,128)(2,1)S(1)} %collective-permute-done.10.refs_1_), channel_id=1, source_target_pairs={{0,64},{1,65},{2,66},{3,67},{4,68},{5,69},{6,70},{7,71},{8,72},{9,... | collective-permute-start | bytes 1572872 | tf_op jit(solution)/shard_map/ppermute | solution.py:38
  78.2 22.6 %collective-permute-start.16 = (bf16[128,2048]{1,0:T(8,128)(2,1)}, bf16[128,2048]{1,0:T(8,128)(2,1)}, u32[]{:S(2)}, u32[]{:S(2)}) collective-permute-start(bf16[128,2048]{1,0:T(8,128)(2,1)} %collective-permute-done.15.refs_6_), channel_id=1, source_target_pairs={{0,192},{1,193},{2,194},{3,195},{4,196},{5,197},{6,198},{7,199},{8... | collective-permute-start | bytes 1572872 | tf_op jit(solution)/shard_map/ppermute | solution.py:38
  89.5 32.0 %collective-permute-start.1 = (bf16[128,2048]{1,0:T(8,128)(2,1)S(1)}, bf16[128,2048]{1,0:T(8,128)(2,1)}, u32[]{:S(2)}, u32[]{:S(2)}) collective-permute-start(bf16[128,2048]{1,0:T(8,128)(2,1)S(1)} %maximum_select_fusion.refs_0_), channel_id=1, source_target_pairs={{0,64},{1,65},{2,66},{3,67},{4,68},{5,69},{6,70},{7,71},{8,72},{9,... | collective-permute-start | bytes 1572872 | tf_op jit(solution)/shard_map/ppermute | solution.py:38
  113.4 27.9 %all-to-all-start.3 = ((bf16[8,128,256]{2,1,0:T(8,128)(2,1)}), bf16[8,128,256]{2,1,0:T(8,128)(2,1)S(1)}, u32[]{:S(2)}, u32[]{:S(2)}) async-start(bf16[8,128,256]{2,1,0:T(8,128)(2,1)} %bitcast.15), calls=%async_computation.3 | async-start | bytes 1048576 | tf_op jit(solution)/shard_map/all_to_all | solution.py:54
  117.9 11.3 %collective-permute-start.2 = (bf16[128,2048]{1,0:T(8,128)(2,1)S(1)}, bf16[128,2048]{1,0:T(8,128)(2,1)S(1)}, u32[]{:S(2)}, u32[]{:S(2)}) collective-permute-start(bf16[128,2048]{1,0:T(8,128)(2,1)S(1)} %maximum_select_fusion.refs_0_), channel_id=1, source_target_pairs={{0,192},{1,193},{2,194},{3,195},{4,196},{5,197},{6,198},{7,199},{8... | collective-permute-start | bytes 1572872 | tf_op jit(solution)/shard_map/ppermute | solution.py:38
  121.4 11.2 %collective-permute-start.3 = (bf16[128,2048]{1,0:T(8,128)(2,1)}, bf16[128,2048]{1,0:T(8,128)(2,1)S(1)}, u32[]{:S(2)}, u32[]{:S(2)}) collective-permute-start(bf16[128,2048]{1,0:T(8,128)(2,1)} %collective-permute-done.1.refs_1_), channel_id=1, source_target_pairs={{0,64},{1,65},{2,66},{3,67},{4,68},{5,69},{6,70},{7,71},{8,72},{9,... | collective-permute-start | bytes 1572872 | tf_op jit(solution)/shard_map/ppermute | solution.py:38
  129.3 3.3 %copy-start.22 = (bf16[128,2048]{1,0:T(8,128)(2,1)}, bf16[128,2048]{1,0:T(8,128)(2,1)S(1)}, u32[]{:S(2)}) copy-start(bf16[128,2048]{1,0:T(8,128)(2,1)S(1)} %collective-permute-done.2.refs_2_) | copy-start | bytes 1572868
  141.3 32.1 %all-to-all-start = ((bf16[8,64,1280]{2,1,0:T(8,128)(2,1)}), bf16[8,64,1280]{2,1,0:T(8,128)(2,1)S(1)}, u32[]{:S(2)}, u32[]{:S(2)}) async-start(bf16[8,64,1280]{2,1,0:T(8,128)(2,1)} %bitcast.13), calls=%async_computation | async-start | bytes 2621440 | tf_op jit(solution)/shard_map/all_to_all | solution.py:54
  146.1 8.0 %collective-permute-start.7 = (bf16[128,2048]{1,0:T(8,128)(2,1)S(1)}, bf16[128,2048]{1,0:T(8,128)(2,1)S(1)}, u32[]{:S(2)}, u32[]{:S(2)}) collective-permute-start(bf16[128,2048]{1,0:T(8,128)(2,1)S(1)} %collective-permute-done.5.refs_0_), channel_id=1, source_target_pairs={{0,192},{1,193},{2,194},{3,195},{4,196},{5,197},{6,198},{7,199},{8... | collective-permute-start | bytes 1572872 | tf_op jit(solution)/shard_map/ppermute | solution.py:38
  146.9 9.8 %collective-permute-start.6 = (bf16[128,2048]{1,0:T(8,128)(2,1)S(1)}, bf16[128,2048]{1,0:T(8,128)(2,1)S(1)}, u32[]{:S(2)}, u32[]{:S(2)}) collective-permute-start(bf16[128,2048]{1,0:T(8,128)(2,1)S(1)} %collective-permute-done.5.refs_0_), channel_id=1, source_target_pairs={{0,64},{1,65},{2,66},{3,67},{4,68},{5,69},{6,70},{7,71},{8,72},{9,... | collective-permute-start | bytes 1572872 | tf_op jit(solution)/shard_map/ppermute | solution.py:38
  154.1 11.3 %copy-start.20 = (bf16[128,2048]{1,0:T(8,128)(2,1)}, bf16[128,2048]{1,0:T(8,128)(2,1)S(1)}, u32[]{:S(2)}) copy-start(bf16[128,2048]{1,0:T(8,128)(2,1)S(1)} %collective-permute-done.7.refs_2_) | copy-start | bytes 1572868
  154.1 11.3 %collective-permute-start.8 = (bf16[128,2048]{1,0:T(8,128)(2,1)S(1)}, bf16[128,2048]{1,0:T(8,128)(2,1)}, u32[]{:S(2)}, u32[]{:S(2)}) collective-permute-start(bf16[128,2048]{1,0:T(8,128)(2,1)S(1)} %collective-permute-done.7.refs_2_), channel_id=1, source_target_pairs={{0,192},{1,193},{2,194},{3,195},{4,196},{5,197},{6,198},{7,199},{8... | collective-permute-start | bytes 1572872 | tf_op jit(solution)/shard_map/ppermute | solution.py:38
  173.4 17.2 %copy-start = (bf16[8,64,1280]{2,1,0:T(8,128)(2,1)}, bf16[8,64,1280]{2,1,0:T(8,128)(2,1)S(1)}, u32[]{:S(2)}) copy-start(bf16[8,64,1280]{2,1,0:T(8,128)(2,1)S(1)} %all-to-all-done.came) | copy-start | bytes 3932164
  190.7 4.0 %copy-start.13 = (s32[512]{0:T(512)S(1)}, s32[512]{0:T(512)}, u32[]{:S(2)}) copy-start(s32[512]{0:T(512)} %param.11) | copy-start | bytes 6148
  190.7 63.6 %all-to-all-start.2 = ((bf16[8,128,1024]{2,1,0:T(8,128)(2,1)}), bf16[8,128,1024]{2,1,0:T(8,128)(2,1)S(1)}, u32[]{:S(2)}, u32[]{:S(2)}) async-start(bf16[8,128,1024]{2,1,0:T(8,128)(2,1)} %bitcast.12), calls=%async_computation.2 | async-start | bytes 4194304 | tf_op jit(solution)/shard_map/all_to_all | solution.py:54
  194.6 2.8 %copy-start.1 = (bf16[8,64,1280]{2,1,0:T(8,128)(2,1)S(1)}, bf16[8,64,1280]{2,1,0:T(8,128)(2,1)}, u32[]{:S(2)}) copy-start(bf16[8,64,1280]{2,1,0:T(8,128)(2,1)} %copy-done) | copy-start | bytes 3932164
  196.7 1.6 copy-start.2
  198.3 0.9 copy-start.5
  198.3 28.9 %copy-start.14 = (s32[8]{0:T(128)S(1)}, s32[8]{0:T(128)}, u32[]{:S(2)}) copy-start(s32[8]{0:T(128)} %param.12) | copy-start | bytes 100
  199.2 5.6 %copy-start.7 = (bf16[64,512]{1,0:T(8,128)(2,1)}, bf16[64,512]{1,0:T(8,128)(2,1)S(1)}, u32[]{:S(2)}) copy-start(bf16[64,512]{1,0:T(8,128)(2,1)S(1)} %get-tuple-element.13) | copy-start | bytes 196612
  199.2 11.7 %copy-start.9 = (bf16[1,256,128]{2,1,0:T(8,128)(2,1)}, bf16[1,256,128]{2,1,0:T(8,128)(2,1)S(1)}, u32[]{:S(2)}) copy-start(bf16[1,256,128]{2,1,0:T(8,128)(2,1)S(1)} %maximum_bitcast_fusion) | copy-start | bytes 196612
  199.2 11.7 %collective-permute-start.19 = (bf16[1,256,128]{2,1,0:T(8,128)(2,1)S(1)}, bf16[1,256,128]{2,1,0:T(8,128)(2,1)S(1)}, u32[]{:S(2)}, u32[]{:S(2)}) collective-permute-start(bf16[1,256,128]{2,1,0:T(8,128)(2,1)S(1)} %maximum_bitcast_fusion), channel_id=1, source_target_pairs={{0,8},{1,9},{2,10},{3,11},{4,12},{5,13},{6,14},{7,15},{8,0},{9,1},... | collective-permute-start | bytes 196616 | tf_op jit(solution)/shard_map/ppermute | solution.py:38
  211.6 14.5 %collective-permute-start.20 = (bf16[2,256,128]{2,1,0:T(8,128)(2,1)S(1)}, bf16[2,256,128]{2,1,0:T(8,128)(2,1)}, u32[]{:S(2)}, u32[]{:S(2)}) collective-permute-start(bf16[2,256,128]{2,1,0:T(8,128)(2,1)S(1)} %pad_maximum_fusion.3), channel_id=1, source_target_pairs={{0,24},{1,25},{2,26},{3,27},{4,28},{5,29},{6,30},{7,31},{8,16},{9,... | collective-permute-start | bytes 393224 | tf_op jit(solution)/shard_map/ppermute | solution.py:38
  227.1 5.4 %collective-permute-start.21 = (bf16[4,256,128]{2,1,0:T(8,128)(2,1)S(1)}, bf16[4,256,128]{2,1,0:T(8,128)(2,1)}, u32[]{:S(2)}, u32[]{:S(2)}) collective-permute-start(bf16[4,256,128]{2,1,0:T(8,128)(2,1)S(1)} %pad_maximum_fusion.own), channel_id=1, source_target_pairs={{0,64},{1,65},{2,66},{3,67},{4,68},{5,69},{6,70},{7,71},{8,72},{9,... | collective-permute-start | bytes 786440 | tf_op jit(solution)/shard_map/ppermute | solution.py:38
  227.3 8.4 %collective-permute-start.22 = (bf16[4,256,128]{2,1,0:T(8,128)(2,1)S(1)}, bf16[4,256,128]{2,1,0:T(8,128)(2,1)}, u32[]{:S(2)}, u32[]{:S(2)}) collective-permute-start(bf16[4,256,128]{2,1,0:T(8,128)(2,1)S(1)} %pad_maximum_fusion.own), channel_id=1, source_target_pairs={{0,192},{1,193},{2,194},{3,195},{4,196},{5,197},{6,198},{7,199},{8... | collective-permute-start | bytes 786440 | tf_op jit(solution)/shard_map/ppermute | solution.py:38
  232.5 7.0 %collective-permute-start.23 = (bf16[4,256,128]{2,1,0:T(8,128)(2,1)}, bf16[4,256,128]{2,1,0:T(8,128)(2,1)}, u32[]{:S(2)}, u32[]{:S(2)}) collective-permute-start(bf16[4,256,128]{2,1,0:T(8,128)(2,1)} %collective-permute-done.21.near), channel_id=1, source_target_pairs={{0,192},{1,193},{2,194},{3,195},{4,196},{5,197},{6,198},{7,199},{8... | collective-permute-start | bytes 786440 | tf_op jit(solution)/shard_map/ppermute | solution.py:38
  239.5 1.0 copy-start.4
  241.9 14.2 %collective-permute-start.24 = (bf16[2,256,256]{2,1,0:T(8,128)(2,1)S(1)}, bf16[2,256,256]{2,1,0:T(8,128)(2,1)}, u32[]{:S(2)}, u32[]{:S(2)}) collective-permute-start(bf16[2,256,256]{2,1,0:T(8,128)(2,1)S(1)} %owned.1.kv), channel_id=1, source_target_pairs={{0,32},{1,33},{2,34},{3,35},{4,36},{5,37},{6,38},{7,39},{8,40},{9,... | collective-permute-start | bytes 786440 | tf_op jit(solution)/shard_map/ppermute | solution.py:38
  254.3 1.8 collective-permute-start.17
  254.3 1.7 copy-start.6
  254.3 1.7 copy-start.8
  255.5 1.6 collective-permute-start.18
  (4 other events, 2.9 us)

commit v3 on v2

--- a/solution.py
+++ b/solution.py
@@ -54,17 +54,14 @@
     return lax.all_to_all(value, axis, 0, 0, tiled=True)
 
 
-def gray(v):
-    return v ^ (v >> 1)
-
-
-def spread_kv(kv):
-    kv = kv[None]
-    for step in (1, 3):
-        kv = jnp.concatenate([kv, send(kv, lambda x, c, zh, step=step: (x, c, zh ^ step))])
-    near = send(kv, lambda x, c, zh: (x ^ 1, c, zh))
-    back = send(kv, lambda x, c, zh: (x ^ 3, c, zh))
-    return kv, near, back, send(near, lambda x, c, zh: (x ^ 3, c, zh))
+def spread_kv(kv, pick):
+    along = [send(kv, along_z(step)) for step in (1, -1, 2)]
+    slots = list(owned(pick, jnp.stack([kv, *along])))
+    for name in ("kx0", "kx1"):
+        for s in range(2):
+            step = 1 if (name == "kx0") == (s == 0) else 3
+            slots[s] = slots[s] + send(slots[s], lambda x, c, zh, step=step: (x ^ step, c, zh))
+    return jnp.stack(slots)
 
 
 def vmem(count):
@@ -266,35 +263,34 @@
     )(rows, *came, *[v for v in tables for _ in parts])
 
 
-def owned_kernel(pick, own, near, back, far, out):
+def owned_kernel(pick, kv, *outs):
     lane = lax.broadcasted_iota(jnp.int32, (64, 128), 1)
     for s in range(2):
-        x_off, odd = pick[4 + 2 * s], pick[5 + 2 * s]
-
-        def part(g, t, x_off=x_off):
+        here, odd = pick[4 + 2 * s] == 0, pick[5 + 2 * s]
+
+        def part(g, t):
             rows = slice(BACK[(t - g) % 4] * 64, BACK[(t - g) % 4] * 64 + 64)
-            got = [v[pick[g], rows, :].astype(F32) for v in (own, near, far, back)]
-            low = jnp.where(x_off == 0, got[0], got[1])
-            return jnp.where(x_off < 2, low, jnp.where(x_off == 2, got[2], got[3]))
+            return kv[pick[g], rows, :].astype(F32)
 
         for t in range(4):
             for half in range(2):
                 a, b = part(2 * half, t), part(2 * half + 1, t)
                 low = jnp.where(odd == 0, a, pltpu.roll(a, 64, 1))
                 high = jnp.where(odd == 0, pltpu.roll(b, 64, 1), b)
-                out[s, t * 64 : (t + 1) * 64, half * 128 : (half + 1) * 128] = jnp.where(lane < 64, low, high).astype(BF16)
-
-
-def owned(pick, arrays):
+                got = jnp.where(here, jnp.where(lane < 64, low, high), 0.0)
+                outs[s][t * 64 : (t + 1) * 64, half * 128 : (half + 1) * 128] = got.astype(BF16)
+
+
+def owned(pick, kv):
     return pl.pallas_call(
         owned_kernel,
-        out_shape=jax.ShapeDtypeStruct((2, 256, 256), BF16),
-        in_specs=[smem()] + vmem(4),
-        out_specs=vmem(1)[0],
+        out_shape=(jax.ShapeDtypeStruct((256, 256), BF16),) * 2,
+        in_specs=[smem()] + vmem(1),
+        out_specs=tuple(vmem(2)),
         cost_estimate=pl.CostEstimate(flops=1 << 20, bytes_accessed=1 << 20, transcendentals=0),
         compiler_params=small(24),
         name="owned",
-    )(pick, *arrays)
+    )(pick, kv)
 
 
 def last_kernel(at, pick, q_near, q_far, q_near_came, q_far_came, kv, kv_came, q_out, kv_out):
@@ -364,7 +360,7 @@
     wanted = lax.dynamic_slice_in_dim(keyval_order, gy * 2, 2, 0)
     four = jnp.arange(4, dtype=jnp.int32)
     pick = jnp.concatenate(
-        [gray(four ^ gy), jnp.stack([wanted // 2 ^ x, wanted % 2], axis=1).reshape(4), core[None]]
+        [jnp.array(BACK, jnp.int32)[(four - gy) % 4], jnp.stack([wanted // 2 ^ x, wanted % 2], axis=1).reshape(4), core[None]]
     )
 
     left, right = send(mine, along_z(1)), send(mine, along_z(-1))
@@ -389,8 +385,7 @@
     q_near = jnp.concatenate(q_own[:2])
     q_near_came = send(jnp.concatenate(q_other[:2]), other_core)
     q_far_came = send(q_other[2], other_core)
-    kv_parts = spread_kv(jnp.concatenate(kvs))
-    kv = owned(pick, kv_parts)
+    kv = spread_kv(jnp.concatenate(kvs), pick)
     kv_came = send(kv, other_core)
     return last(at, pick, (q_near, q_own[2], q_near_came, q_far_came, kv, kv_came), tokens)
 

time: 260 us -> 253 us (0.973)
  starting transfers between devices: 80.3 us -> 77.3 us
    ppermute x25 -> x27, starting transfers between devices: 67 us -> 63.7 us  [send(): return lax.ppermute(value, AXES, moves(rule))]
    unnamed x49 -> x39, local copies, waits for them, and re-layouts: 5.88 us -> 2.82 us
    ppermute x25 -> x27, waiting for transfers between devices: 108 us -> 109 us  [send(): return lax.ppermute(value, AXES, moves(rule))]
  transfers between devices with their start and end apart: 28 -> 30, of which waited for: 17 -> 18; matrix products, arithmetic and copies ran while one was open for 2% -> 2% of each run, Pallas kernels for 13% -> 13%
where the time goes in v3:
time: 253 us
  waiting for transfers between devices  109 us (43%)
  starting transfers between devices  77.3 us (31%)
  Pallas kernels  38.9 us (15%)
  blocking collectives  17.1 us (7%)
  local copies, waits for them, and re-layouts  5.02 us (2%)
  other arithmetic  4.49 us (2%)
    ppermute x27, waiting for transfers between devices, send(): return lax.ppermute(value, AXES, moves(rule))  109 us
    ppermute x27, starting transfers between devices, send(): return lax.ppermute(value, AXES, moves(rule))  63.7 us
    pallas_call x3, Pallas kernels, project(): pl.pallas_call(functools.partial(project_kernel, count), out_shape=tuple(...  28.3 us
    all_to_all x1, blocking collectives, exchange(): return lax.all_to_all(value, axis, 0, 0, tiled=True)  17.1 us
    all_to_all x3, starting transfers between devices, exchange(): return lax.all_to_all(value, axis, 0, 0, tiled=True)  13.6 us
  transfers between devices with their start and end apart: 30, of which 18 were waited for; matrix products, arithmetic and copies ran while one was open for 2% of the time, Pallas kernels for 13%

profile of v3, /device:TPU:1, one launch (start us, length us, event | category | flops | bytes accessed | tf_op | source)
XLA Modules:
  0.0 252.8 jit_solution(6363457612211175574)
XLA Ops:
  1.3 1.4 copy.14.gain
  2.7 2.0 copy.13.wk
  4.6 4.3 %prepare.1.refs_4_.refs_8_ = bf16[2048,640]{1,0:T(8,128)(2,1)} custom-call(bf16[2048,512]{1,0:T(8,128)(2,1)} %wq.1, bf16[2048,64]{1,0:T(8,128)(2,1)} %copy.13.wk, f32[2048,1]{1,0:T(8,128)} %copy.14.gain), custom_call_target="tpu_custom_call" | custom-call | flops 1048576 | bytes 5242880 | tf_op jit(solution)/shard_map/prepare/pallas_call | solution.py:86
  9.0 3.2 %collective-permute-start.4 = (bf16[2048,640]{1,0:T(8,128)(2,1)}, bf16[2048,640]{1,0:T(8,128)(2,1)}, u32[]{:S(2)}, u32[]{:S(2)}) collective-permute-start(bf16[2048,640]{1,0:T(8,128)(2,1)} %prepare.1.refs_4_.refs_8_), channel_id=1, source_target_pairs={{0,32},{1,33},{2,34},{3,35},{4,36},{5,37},{6,38},{7,39},{8,40},{9,... | collective-permute-start | bytes 7864328 | tf_op jit(solution)/shard_map/ppermute | solution.py:38
  12.3 5.0 %collective-permute-done = bf16[64,2048]{1,0:T(8,128)(2,1)S(1)} collective-permute-done((bf16[64,2048]{1,0:T(8,128)(2,1)S(1)}, bf16[64,2048]{1,0:T(8,128)(2,1)S(1)}, u32[]{:S(2)}, u32[]{:S(2)}) %collective-permute-start) | collective-permute-done | bytes 262176 | tf_op jit(solution)/shard_map/ppermute | solution.py:38
  17.4 1.4 collective-permute-start.5
  18.8 3.1 %collective-permute-start.9 = (bf16[128,2048]{1,0:T(8,128)(2,1)S(1)}, bf16[128,2048]{1,0:T(8,128)(2,1)S(1)}, u32[]{:S(2)}, u32[]{:S(2)}) collective-permute-start(bf16[128,2048]{1,0:T(8,128)(2,1)S(1)} %maximum_select_fusion.refs_0_), channel_id=1, source_target_pairs={{0,24},{1,25},{2,26},{3,27},{4,28},{5,29},{6,30},{7,31},{8,0},{9,1... | collective-permute-start | bytes 1572872 | tf_op jit(solution)/shard_map/ppermute | solution.py:38
  21.9 16.2 %collective-permute-done.5.refs_0_ = bf16[128,2048]{1,0:T(8,128)(2,1)S(1)} collective-permute-done((bf16[128,2048]{1,0:T(8,128)(2,1)S(1)}, bf16[128,2048]{1,0:T(8,128)(2,1)S(1)}, u32[]{:S(2)}, u32[]{:S(2)}) %collective-permute-start.5) | collective-permute-done | bytes 524320 | tf_op jit(solution)/shard_map/ppermute | solution.py:38
  38.1 7.3 %collective-permute-start.13 = (bf16[128,2048]{1,0:T(8,128)(2,1)S(1)}, bf16[128,2048]{1,0:T(8,128)(2,1)}, u32[]{:S(2)}, u32[]{:S(2)}) collective-permute-start(bf16[128,2048]{1,0:T(8,128)(2,1)S(1)} %collective-permute-done.5.refs_0_), channel_id=1, source_target_pairs={{0,8},{1,9},{2,10},{3,11},{4,12},{5,13},{6,14},{7,15},{8,16},{9,17... | collective-permute-start | bytes 1572872 | tf_op jit(solution)/shard_map/ppermute | solution.py:38
  46.1 1.2 collective-permute-start.10
  47.4 19.7 %collective-permute-done.13.refs_4_ = bf16[128,2048]{1,0:T(8,128)(2,1)} collective-permute-done((bf16[128,2048]{1,0:T(8,128)(2,1)S(1)}, bf16[128,2048]{1,0:T(8,128)(2,1)}, u32[]{:S(2)}, u32[]{:S(2)}) %collective-permute-start.13) | collective-permute-done | bytes 524320 | tf_op jit(solution)/shard_map/ppermute | solution.py:38
  67.0 2.5 collective-permute-start.15
  70.1 0.9 collective-permute-start.14
  71.0 7.3 %collective-permute-done.15.refs_6_ = bf16[128,2048]{1,0:T(8,128)(2,1)} collective-permute-done((bf16[128,2048]{1,0:T(8,128)(2,1)}, bf16[128,2048]{1,0:T(8,128)(2,1)}, u32[]{:S(2)}, u32[]{:S(2)}) %collective-permute-start.15) | collective-permute-done | bytes 524320 | tf_op jit(solution)/shard_map/ppermute | solution.py:38
  78.3 3.4 %collective-permute-start.16 = (bf16[128,2048]{1,0:T(8,128)(2,1)}, bf16[128,2048]{1,0:T(8,128)(2,1)}, u32[]{:S(2)}, u32[]{:S(2)}) collective-permute-start(bf16[128,2048]{1,0:T(8,128)(2,1)} %collective-permute-done.15.refs_6_), channel_id=1, source_target_pairs={{0,192},{1,193},{2,194},{3,195},{4,196},{5,197},{6,198},{7,199},{8... | collective-permute-start | bytes 1572872 | tf_op jit(solution)/shard_map/ppermute | solution.py:38
  82.3 7.1 %collective-permute-done.11.refs_2_ = bf16[128,2048]{1,0:T(8,128)(2,1)} collective-permute-done((bf16[128,2048]{1,0:T(8,128)(2,1)S(1)}, bf16[128,2048]{1,0:T(8,128)(2,1)}, u32[]{:S(2)}, u32[]{:S(2)}) %collective-permute-start.11) | collective-permute-done | bytes 524320 | tf_op jit(solution)/shard_map/ppermute | solution.py:38
  89.4 1.0 collective-permute-start.1
  90.5 2.5 collective-permute-done.12.refs_3_
  92.9 7.8 %collective-permute-done.16.refs_7_ = bf16[128,2048]{1,0:T(8,128)(2,1)} collective-permute-done((bf16[128,2048]{1,0:T(8,128)(2,1)}, bf16[128,2048]{1,0:T(8,128)(2,1)}, u32[]{:S(2)}, u32[]{:S(2)}) %collective-permute-start.16) | collective-permute-done | bytes 524320 | tf_op jit(solution)/shard_map/ppermute | solution.py:38
  100.8 12.5 %shard_map.99 = (bf16[1024,1024]{1,0:T(8,128)(2,1)}, bf16[1024,256]{1,0:T(8,128)(2,1)}) custom-call(s32[5]{0:T(128)} %pad_add_fusion.3.at, bf16[128,2048]{1,0:T(8,128)(2,1)} %copy-done.14, bf16[128,2048]{1,0:T(8,128)(2,1)} %collective-permute-done.10.refs_1_, bf16[128,2048]{1,0:T(8,128)(2,1)} %collective-permute-done.11.refs_2_, ...), custom_call_target="tpu_custom_call" | custom-call | flops 4831838208 | bytes 11534336 | tf_op jit(solution)/shard_map/pallas_call | solution.py:171
  113.3 4.8 %all-to-all-start.3 = ((bf16[8,128,256]{2,1,0:T(8,128)(2,1)}), bf16[8,128,256]{2,1,0:T(8,128)(2,1)S(1)}, u32[]{:S(2)}, u32[]{:S(2)}) async-start(bf16[8,128,256]{2,1,0:T(8,128)(2,1)} %bitcast.24), calls=%async_computation.3 | async-start | bytes 1048576 | tf_op jit(solution)/shard_map/all_to_all | solution.py:54
  118.1 3.5 %collective-permute-start.2 = (bf16[128,2048]{1,0:T(8,128)(2,1)S(1)}, bf16[128,2048]{1,0:T(8,128)(2,1)S(1)}, u32[]{:S(2)}, u32[]{:S(2)}) collective-permute-start(bf16[128,2048]{1,0:T(8,128)(2,1)S(1)} %maximum_select_fusion.refs_0_), channel_id=1, source_target_pairs={{0,192},{1,193},{2,194},{3,195},{4,196},{5,197},{6,198},{7,199},{8... | collective-permute-start | bytes 1572872 | tf_op jit(solution)/shard_map/ppermute | solution.py:38
  121.6 7.9 %collective-permute-done.2.refs_2_ = bf16[128,2048]{1,0:T(8,128)(2,1)S(1)} collective-permute-done((bf16[128,2048]{1,0:T(8,128)(2,1)S(1)}, bf16[128,2048]{1,0:T(8,128)(2,1)S(1)}, u32[]{:S(2)}, u32[]{:S(2)}) %collective-permute-start.2) | collective-permute-done | bytes 524320 | tf_op jit(solution)/shard_map/ppermute | solution.py:38
  129.5 3.2 %collective-permute-done.3.refs_3_ = bf16[128,2048]{1,0:T(8,128)(2,1)} collective-permute-done((bf16[128,2048]{1,0:T(8,128)(2,1)S(1)}, bf16[128,2048]{1,0:T(8,128)(2,1)}, u32[]{:S(2)}, u32[]{:S(2)}) %collective-permute-start.3) | collective-permute-done | bytes 524320 | tf_op jit(solution)/shard_map/ppermute | solution.py:38
  132.7 7.9 %shard_map.95 = bf16[512,1280]{1,0:T(8,128)(2,1)} custom-call(s32[5]{0:T(128)} %pad_add_fusion.3.at, bf16[128,2048]{1,0:T(8,128)(2,1)} %copy-done.9, bf16[128,2048]{1,0:T(8,128)(2,1)} %copy-done.15, bf16[128,2048]{1,0:T(8,128)(2,1)} %copy-done.18, bf16[128,2048]{1,0:T(8,128)(2,1)} %collective-permute-done.3.refs_3_, ...), custom_call_target="tpu_custom_call" | custom-call | flops 2415919104 | bytes 8388608 | tf_op jit(solution)/shard_map/pallas_call | solution.py:171
  140.7 4.8 %all-to-all-start = ((bf16[8,64,1280]{2,1,0:T(8,128)(2,1)}), bf16[8,64,1280]{2,1,0:T(8,128)(2,1)S(1)}, u32[]{:S(2)}, u32[]{:S(2)}) async-start(bf16[8,64,1280]{2,1,0:T(8,128)(2,1)} %bitcast.22), calls=%async_computation | async-start | bytes 2621440 | tf_op jit(solution)/shard_map/all_to_all | solution.py:54
  145.5 1.0 collective-permute-start.7
  146.9 7.0 %collective-permute-done.7.refs_2_ = bf16[128,2048]{1,0:T(8,128)(2,1)S(1)} collective-permute-done((bf16[128,2048]{1,0:T(8,128)(2,1)S(1)}, bf16[128,2048]{1,0:T(8,128)(2,1)S(1)}, u32[]{:S(2)}, u32[]{:S(2)}) %collective-permute-start.7) | collective-permute-done | bytes 524320 | tf_op jit(solution)/shard_map/ppermute | solution.py:38
  153.9 2.5 collective-permute-start.8
  157.1 7.7 %collective-permute-done.8.refs_3_ = bf16[128,2048]{1,0:T(8,128)(2,1)} collective-permute-done((bf16[128,2048]{1,0:T(8,128)(2,1)S(1)}, bf16[128,2048]{1,0:T(8,128)(2,1)}, u32[]{:S(2)}, u32[]{:S(2)}) %collective-permute-start.8) | collective-permute-done | bytes 524320 | tf_op jit(solution)/shard_map/ppermute | solution.py:38
  164.8 7.9 %shard_map.97 = bf16[512,1280]{1,0:T(8,128)(2,1)} custom-call(s32[5]{0:T(128)} %pad_add_fusion.3.at, bf16[128,2048]{1,0:T(8,128)(2,1)} %copy-done.13, bf16[128,2048]{1,0:T(8,128)(2,1)} %copy-done.17, bf16[128,2048]{1,0:T(8,128)(2,1)} %copy-done.16, bf16[128,2048]{1,0:T(8,128)(2,1)} %collective-permute-done.8.refs_3_, ...), custom_call_target="tpu_custom_call" | custom-call | flops 2415919104 | bytes 8388608 | tf_op jit(solution)/shard_map/pallas_call | solution.py:171
  172.7 17.1 %all_to_all.20.came = bf16[8,64,1280]{2,1,0:T(8,128)(2,1)} all-to-all(bf16[8,64,1280]{2,1,0:T(8,128)(2,1)} %bitcast.23), channel_id=1, replica_groups=mesh['gx'=8,'gy'=4,'gz'=8] {'gz'}, dimensions={0} | all-to-all | bytes 2621440 | tf_op jit(solution)/shard_map/all_to_all | solution.py:54
  189.9 4.0 %all-to-all-start.2 = ((bf16[8,128,1024]{2,1,0:T(8,128)(2,1)}), bf16[8,128,1024]{2,1,0:T(8,128)(2,1)S(1)}, u32[]{:S(2)}, u32[]{:S(2)}) async-start(bf16[8,128,1024]{2,1,0:T(8,128)(2,1)} %bitcast.21), calls=%async_computation.2 | async-start | bytes 4194304 | tf_op jit(solution)/shard_map/all_to_all | solution.py:54
  195.0 1.9 fusion.3
  199.4 5.4 %collective-permute-start.19 = (bf16[256,128]{1,0:T(8,128)(2,1)S(1)}, bf16[256,128]{1,0:T(8,128)(2,1)S(1)}, u32[]{:S(2)}, u32[]{:S(2)}) collective-permute-start(bf16[256,128]{1,0:T(8,128)(2,1)S(1)} %get-tuple-element.33), channel_id=1, source_target_pairs={{0,8},{1,9},{2,10},{3,11},{4,12},{5,13},{6,14},{7,15},{8,16},{9,17... | collective-permute-start | bytes 196616 | tf_op jit(solution)/shard_map/ppermute | solution.py:38
  204.8 1.9 collective-permute-start.20
  206.8 5.8 %collective-permute-start.21 = (bf16[256,128]{1,0:T(8,128)(2,1)S(1)}, bf16[256,128]{1,0:T(8,128)(2,1)S(1)}, u32[]{:S(2)}, u32[]{:S(2)}) collective-permute-start(bf16[256,128]{1,0:T(8,128)(2,1)S(1)} %get-tuple-element.33), channel_id=1, source_target_pairs={{0,16},{1,17},{2,18},{3,19},{4,20},{5,21},{6,22},{7,23},{8,24},{9,... | collective-permute-start | bytes 196616 | tf_op jit(solution)/shard_map/ppermute | solution.py:38
  212.6 7.5 %collective-permute-done.19 = bf16[256,128]{1,0:T(8,128)(2,1)S(1)} collective-permute-done((bf16[256,128]{1,0:T(8,128)(2,1)S(1)}, bf16[256,128]{1,0:T(8,128)(2,1)S(1)}, u32[]{:S(2)}, u32[]{:S(2)}) %collective-permute-start.19) | collective-permute-done | bytes 65568 | tf_op jit(solution)/shard_map/ppermute | solution.py:38
  220.1 3.7 %collective-permute-done.21 = bf16[256,128]{1,0:T(8,128)(2,1)S(1)} collective-permute-done((bf16[256,128]{1,0:T(8,128)(2,1)S(1)}, bf16[256,128]{1,0:T(8,128)(2,1)S(1)}, u32[]{:S(2)}, u32[]{:S(2)}) %collective-permute-start.21) | collective-permute-done | bytes 65568 | tf_op jit(solution)/shard_map/ppermute | solution.py:38
  224.7 3.1 %collective-permute-start.24 = (bf16[256,256]{1,0:T(8,128)(2,1)S(1)}, bf16[256,256]{1,0:T(8,128)(2,1)S(1)}, u32[]{:S(2)}, u32[]{:S(2)}) collective-permute-start(bf16[256,256]{1,0:T(8,128)(2,1)S(1)} %get-tuple-element.25), channel_id=1, source_target_pairs={{0,192},{1,193},{2,194},{3,195},{4,196},{5,197},{6,198},{7,199},{8... | collective-permute-start | bytes 393224 | tf_op jit(solution)/shard_map/ppermute | solution.py:38
  227.8 1.0 collective-permute-done.22
  228.8 3.1 %collective-permute-start.23 = (bf16[256,256]{1,0:T(8,128)(2,1)S(1)}, bf16[256,256]{1,0:T(8,128)(2,1)S(1)}, u32[]{:S(2)}, u32[]{:S(2)}) collective-permute-start(bf16[256,256]{1,0:T(8,128)(2,1)S(1)} %add.171), channel_id=1, source_target_pairs={{0,192},{1,193},{2,194},{3,195},{4,196},{5,197},{6,198},{7,199},{8... | collective-permute-start | bytes 393224 | tf_op jit(solution)/shard_map/ppermute | solution.py:38
  232.1 2.2 collective-permute-done.23
  234.3 1.6 collective-permute-done.25
  235.9 11.5 %collective-permute-start.26 = (bf16[2,256,256]{2,1,0:T(8,128)(2,1)S(1)}, bf16[2,256,256]{2,1,0:T(8,128)(2,1)}, u32[]{:S(2)}, u32[]{:S(2)}) collective-permute-start(bf16[2,256,256]{2,1,0:T(8,128)(2,1)S(1)} %pad_maximum_fusion.1.kv), channel_id=1, source_target_pairs={{0,32},{1,33},{2,34},{3,35},{4,36},{5,37},{6,38},{7,39},{8,40},{9,... | collective-permute-start | bytes 786440 | tf_op jit(solution)/shard_map/ppermute | solution.py:38
  248.1 1.1 shard_map.100
  249.9 0.9 collective-permute-done.18.q_far_came
  250.8 2.0 last.1
  (92 shorter events, 10.1 us)
Async XLA Ops:
  4.6 7.6 %copy-start.8 = (bf16[128,2048]{1,0:T(8,128)(2,1)S(1)}, bf16[128,2048]{1,0:T(8,128)(2,1)}, u32[]{:S(2)}) copy-start(bf16[128,2048]{1,0:T(8,128)(2,1)} %param.8) | copy-start | bytes 1572868
  9.0 72.7 %copy-start.12 = (s32[4]{0:T(128)S(1)}, s32[4]{0:T(128)}, u32[]{:S(2)}) copy-start(s32[4]{0:T(128)} %constant.147.clone) | copy-start | bytes 52
  9.0 91.8 %collective-permute-start.4 = (bf16[2048,640]{1,0:T(8,128)(2,1)}, bf16[2048,640]{1,0:T(8,128)(2,1)}, u32[]{:S(2)}, u32[]{:S(2)}) collective-permute-start(bf16[2048,640]{1,0:T(8,128)(2,1)} %prepare.1.refs_4_.refs_8_), channel_id=1, source_target_pairs={{0,32},{1,33},{2,34},{3,35},{4,36},{5,37},{6,38},{7,39},{8,40},{9,... | collective-permute-start | bytes 7864328 | tf_op jit(solution)/shard_map/ppermute | solution.py:38
  12.2 5.1 %collective-permute-start = (bf16[64,2048]{1,0:T(8,128)(2,1)S(1)}, bf16[64,2048]{1,0:T(8,128)(2,1)S(1)}, u32[]{:S(2)}, u32[]{:S(2)}) collective-permute-start(bf16[64,2048]{1,0:T(8,128)(2,1)S(1)} %get-tuple-element.31), channel_id=1, source_target_pairs={{0,32},{1,33},{2,34},{3,35},{4,36},{5,37},{6,38},{7,39},{8,40},{9,... | collective-permute-start | bytes 786440 | tf_op jit(solution)/shard_map/ppermute | solution.py:38
  17.4 100.7 %copy-start.9 = (bf16[128,2048]{1,0:T(8,128)(2,1)}, bf16[128,2048]{1,0:T(8,128)(2,1)S(1)}, u32[]{:S(2)}) copy-start(bf16[128,2048]{1,0:T(8,128)(2,1)S(1)} %maximum_select_fusion.refs_0_) | copy-start | bytes 1572868
  17.4 20.7 %collective-permute-start.5 = (bf16[128,2048]{1,0:T(8,128)(2,1)S(1)}, bf16[128,2048]{1,0:T(8,128)(2,1)S(1)}, u32[]{:S(2)}, u32[]{:S(2)}) collective-permute-start(bf16[128,2048]{1,0:T(8,128)(2,1)S(1)} %maximum_select_fusion.refs_0_), channel_id=1, source_target_pairs={{0,8},{1,9},{2,10},{3,11},{4,12},{5,13},{6,14},{7,15},{8,16},{9,17... | collective-permute-start | bytes 1572872 | tf_op jit(solution)/shard_map/ppermute | solution.py:38
  18.8 27.4 %collective-permute-start.9 = (bf16[128,2048]{1,0:T(8,128)(2,1)S(1)}, bf16[128,2048]{1,0:T(8,128)(2,1)S(1)}, u32[]{:S(2)}, u32[]{:S(2)}) collective-permute-start(bf16[128,2048]{1,0:T(8,128)(2,1)S(1)} %maximum_select_fusion.refs_0_), channel_id=1, source_target_pairs={{0,24},{1,25},{2,26},{3,27},{4,28},{5,29},{6,30},{7,31},{8,0},{9,1... | collective-permute-start | bytes 1572872 | tf_op jit(solution)/shard_map/ppermute | solution.py:38
  38.1 108.3 %copy-start.13 = (bf16[128,2048]{1,0:T(8,128)(2,1)}, bf16[128,2048]{1,0:T(8,128)(2,1)S(1)}, u32[]{:S(2)}) copy-start(bf16[128,2048]{1,0:T(8,128)(2,1)S(1)} %collective-permute-done.5.refs_0_) | copy-start | bytes 1572868
  38.1 28.9 %collective-permute-start.13 = (bf16[128,2048]{1,0:T(8,128)(2,1)S(1)}, bf16[128,2048]{1,0:T(8,128)(2,1)}, u32[]{:S(2)}, u32[]{:S(2)}) collective-permute-start(bf16[128,2048]{1,0:T(8,128)(2,1)S(1)} %collective-permute-done.5.refs_0_), channel_id=1, source_target_pairs={{0,8},{1,9},{2,10},{3,11},{4,12},{5,13},{6,14},{7,15},{8,16},{9,17... | collective-permute-start | bytes 1572872 | tf_op jit(solution)/shard_map/ppermute | solution.py:38
  46.1 54.6 %copy-start.14 = (bf16[128,2048]{1,0:T(8,128)(2,1)}, bf16[128,2048]{1,0:T(8,128)(2,1)S(1)}, u32[]{:S(2)}) copy-start(bf16[128,2048]{1,0:T(8,128)(2,1)S(1)} %collective-permute-done.9.refs_0_) | copy-start | bytes 1572868
  46.1 24.8 %collective-permute-start.10 = (bf16[128,2048]{1,0:T(8,128)(2,1)S(1)}, bf16[128,2048]{1,0:T(8,128)(2,1)}, u32[]{:S(2)}, u32[]{:S(2)}) collective-permute-start(bf16[128,2048]{1,0:T(8,128)(2,1)S(1)} %collective-permute-done.9.refs_0_), channel_id=1, source_target_pairs={{0,64},{1,65},{2,66},{3,67},{4,68},{5,69},{6,70},{7,71},{8,72},{9,... | collective-permute-start | bytes 1572872 | tf_op jit(solution)/shard_map/ppermute | solution.py:38
  67.0 11.3 %collective-permute-start.15 = (bf16[128,2048]{1,0:T(8,128)(2,1)}, bf16[128,2048]{1,0:T(8,128)(2,1)}, u32[]{:S(2)}, u32[]{:S(2)}) collective-permute-start(bf16[128,2048]{1,0:T(8,128)(2,1)} %collective-permute-done.13.refs_4_), channel_id=1, source_target_pairs={{0,192},{1,193},{2,194},{3,195},{4,196},{5,197},{6,198},{7,199},{8... | collective-permute-start | bytes 1572872 | tf_op jit(solution)/shard_map/ppermute | solution.py:38
  69.5 19.9 %collective-permute-start.11 = (bf16[128,2048]{1,0:T(8,128)(2,1)S(1)}, bf16[128,2048]{1,0:T(8,128)(2,1)}, u32[]{:S(2)}, u32[]{:S(2)}) collective-permute-start(bf16[128,2048]{1,0:T(8,128)(2,1)S(1)} %collective-permute-done.9.refs_0_), channel_id=1, source_target_pairs={{0,192},{1,193},{2,194},{3,195},{4,196},{5,197},{6,198},{7,199},{8... | collective-permute-start | bytes 1572872 | tf_op jit(solution)/shard_map/ppermute | solution.py:38
  70.1 22.9 %collective-permute-start.14 = (bf16[128,2048]{1,0:T(8,128)(2,1)}, bf16[128,2048]{1,0:T(8,128)(2,1)}, u32[]{:S(2)}, u32[]{:S(2)}) collective-permute-start(bf16[128,2048]{1,0:T(8,128)(2,1)} %collective-permute-done.13.refs_4_), channel_id=1, source_target_pairs={{0,64},{1,65},{2,66},{3,67},{4,68},{5,69},{6,70},{7,71},{8,72},{9,... | collective-permute-start | bytes 1572872 | tf_op jit(solution)/shard_map/ppermute | solution.py:38
  71.0 21.9 %collective-permute-start.12 = (bf16[128,2048]{1,0:T(8,128)(2,1)}, bf16[128,2048]{1,0:T(8,128)(2,1)}, u32[]{:S(2)}, u32[]{:S(2)}) collective-permute-start(bf16[128,2048]{1,0:T(8,128)(2,1)} %collective-permute-done.10.refs_1_), channel_id=1, source_target_pairs={{0,64},{1,65},{2,66},{3,67},{4,68},{5,69},{6,70},{7,71},{8,72},{9,... | collective-permute-start | bytes 1572872 | tf_op jit(solution)/shard_map/ppermute | solution.py:38
  78.3 22.5 %collective-permute-start.16 = (bf16[128,2048]{1,0:T(8,128)(2,1)}, bf16[128,2048]{1,0:T(8,128)(2,1)}, u32[]{:S(2)}, u32[]{:S(2)}) collective-permute-start(bf16[128,2048]{1,0:T(8,128)(2,1)} %collective-permute-done.15.refs_6_), channel_id=1, source_target_pairs={{0,192},{1,193},{2,194},{3,195},{4,196},{5,197},{6,198},{7,199},{8... | collective-permute-start | bytes 1572872 | tf_op jit(solution)/shard_map/ppermute | solution.py:38
  89.4 32.1 %collective-permute-start.1 = (bf16[128,2048]{1,0:T(8,128)(2,1)S(1)}, bf16[128,2048]{1,0:T(8,128)(2,1)S(1)}, u32[]{:S(2)}, u32[]{:S(2)}) collective-permute-start(bf16[128,2048]{1,0:T(8,128)(2,1)S(1)} %maximum_select_fusion.refs_0_), channel_id=1, source_target_pairs={{0,64},{1,65},{2,66},{3,67},{4,68},{5,69},{6,70},{7,71},{8,72},{9,... | collective-permute-start | bytes 1572872 | tf_op jit(solution)/shard_map/ppermute | solution.py:38
  113.3 27.4 %all-to-all-start.3 = ((bf16[8,128,256]{2,1,0:T(8,128)(2,1)}), bf16[8,128,256]{2,1,0:T(8,128)(2,1)S(1)}, u32[]{:S(2)}, u32[]{:S(2)}) async-start(bf16[8,128,256]{2,1,0:T(8,128)(2,1)} %bitcast.24), calls=%async_computation.3 | async-start | bytes 1048576 | tf_op jit(solution)/shard_map/all_to_all | solution.py:54
  118.1 11.4 %collective-permute-start.2 = (bf16[128,2048]{1,0:T(8,128)(2,1)S(1)}, bf16[128,2048]{1,0:T(8,128)(2,1)S(1)}, u32[]{:S(2)}, u32[]{:S(2)}) collective-permute-start(bf16[128,2048]{1,0:T(8,128)(2,1)S(1)} %maximum_select_fusion.refs_0_), channel_id=1, source_target_pairs={{0,192},{1,193},{2,194},{3,195},{4,196},{5,197},{6,198},{7,199},{8... | collective-permute-start | bytes 1572872 | tf_op jit(solution)/shard_map/ppermute | solution.py:38
  121.6 11.2 %copy-start.15 = (bf16[128,2048]{1,0:T(8,128)(2,1)}, bf16[128,2048]{1,0:T(8,128)(2,1)S(1)}, u32[]{:S(2)}) copy-start(bf16[128,2048]{1,0:T(8,128)(2,1)S(1)} %collective-permute-done.1.refs_1_) | copy-start | bytes 1572868
  121.6 11.2 %collective-permute-start.3 = (bf16[128,2048]{1,0:T(8,128)(2,1)S(1)}, bf16[128,2048]{1,0:T(8,128)(2,1)}, u32[]{:S(2)}, u32[]{:S(2)}) collective-permute-start(bf16[128,2048]{1,0:T(8,128)(2,1)S(1)} %collective-permute-done.1.refs_1_), channel_id=1, source_target_pairs={{0,64},{1,65},{2,66},{3,67},{4,68},{5,69},{6,70},{7,71},{8,72},{9,... | collective-permute-start | bytes 1572872 | tf_op jit(solution)/shard_map/ppermute | solution.py:38
  129.5 3.2 %copy-start.18 = (bf16[128,2048]{1,0:T(8,128)(2,1)}, bf16[128,2048]{1,0:T(8,128)(2,1)S(1)}, u32[]{:S(2)}) copy-start(bf16[128,2048]{1,0:T(8,128)(2,1)S(1)} %collective-permute-done.2.refs_2_) | copy-start | bytes 1572868
  140.7 32.0 %all-to-all-start = ((bf16[8,64,1280]{2,1,0:T(8,128)(2,1)}), bf16[8,64,1280]{2,1,0:T(8,128)(2,1)S(1)}, u32[]{:S(2)}, u32[]{:S(2)}) async-start(bf16[8,64,1280]{2,1,0:T(8,128)(2,1)} %bitcast.22), calls=%async_computation | async-start | bytes 2621440 | tf_op jit(solution)/shard_map/all_to_all | solution.py:54
  145.5 8.4 %collective-permute-start.7 = (bf16[128,2048]{1,0:T(8,128)(2,1)S(1)}, bf16[128,2048]{1,0:T(8,128)(2,1)S(1)}, u32[]{:S(2)}, u32[]{:S(2)}) collective-permute-start(bf16[128,2048]{1,0:T(8,128)(2,1)S(1)} %collective-permute-done.5.refs_0_), channel_id=1, source_target_pairs={{0,192},{1,193},{2,194},{3,195},{4,196},{5,197},{6,198},{7,199},{8... | collective-permute-start | bytes 1572872 | tf_op jit(solution)/shard_map/ppermute | solution.py:38
  146.4 9.9 %collective-permute-start.6 = (bf16[128,2048]{1,0:T(8,128)(2,1)S(1)}, bf16[128,2048]{1,0:T(8,128)(2,1)S(1)}, u32[]{:S(2)}, u32[]{:S(2)}) collective-permute-start(bf16[128,2048]{1,0:T(8,128)(2,1)S(1)} %collective-permute-done.5.refs_0_), channel_id=1, source_target_pairs={{0,64},{1,65},{2,66},{3,67},{4,68},{5,69},{6,70},{7,71},{8,72},{9,... | collective-permute-start | bytes 1572872 | tf_op jit(solution)/shard_map/ppermute | solution.py:38
  153.9 10.9 %copy-start.16 = (bf16[128,2048]{1,0:T(8,128)(2,1)}, bf16[128,2048]{1,0:T(8,128)(2,1)S(1)}, u32[]{:S(2)}) copy-start(bf16[128,2048]{1,0:T(8,128)(2,1)S(1)} %collective-permute-done.7.refs_2_) | copy-start | bytes 1572868
  153.9 10.9 %collective-permute-start.8 = (bf16[128,2048]{1,0:T(8,128)(2,1)S(1)}, bf16[128,2048]{1,0:T(8,128)(2,1)}, u32[]{:S(2)}, u32[]{:S(2)}) collective-permute-start(bf16[128,2048]{1,0:T(8,128)(2,1)S(1)} %collective-permute-done.7.refs_2_), channel_id=1, source_target_pairs={{0,192},{1,193},{2,194},{3,195},{4,196},{5,197},{6,198},{7,199},{8... | collective-permute-start | bytes 1572872 | tf_op jit(solution)/shard_map/ppermute | solution.py:38
  172.7 17.1 %copy-start = (bf16[8,64,1280]{2,1,0:T(8,128)(2,1)}, bf16[8,64,1280]{2,1,0:T(8,128)(2,1)S(1)}, u32[]{:S(2)}) copy-start(bf16[8,64,1280]{2,1,0:T(8,128)(2,1)S(1)} %all-to-all-done.came) | copy-start | bytes 3932164
  189.9 4.0 %copy-start.10 = (s32[512]{0:T(512)S(1)}, s32[512]{0:T(512)}, u32[]{:S(2)}) copy-start(s32[512]{0:T(512)} %param.12) | copy-start | bytes 6148
  189.9 4.0 %copy-start.11 = (s32[8]{0:T(128)S(1)}, s32[8]{0:T(128)}, u32[]{:S(2)}) copy-start(s32[8]{0:T(128)} %param.13) | copy-start | bytes 100
  189.9 4.3 %copy-start.7 = (s32[4]{0:T(128)S(1)}, s32[4]{0:T(128)}, u32[]{:S(2)}) copy-start(s32[4]{0:T(128)} %constant.148.clone) | copy-start | bytes 52
  189.9 58.2 %all-to-all-start.2 = ((bf16[8,128,1024]{2,1,0:T(8,128)(2,1)}), bf16[8,128,1024]{2,1,0:T(8,128)(2,1)S(1)}, u32[]{:S(2)}, u32[]{:S(2)}) async-start(bf16[8,128,1024]{2,1,0:T(8,128)(2,1)} %bitcast.21), calls=%async_computation.2 | async-start | bytes 4194304 | tf_op jit(solution)/shard_map/all_to_all | solution.py:54
  194.9 2.8 %copy-start.1 = (bf16[8,64,1280]{2,1,0:T(8,128)(2,1)S(1)}, bf16[8,64,1280]{2,1,0:T(8,128)(2,1)}, u32[]{:S(2)}) copy-start(bf16[8,64,1280]{2,1,0:T(8,128)(2,1)} %copy-done) | copy-start | bytes 3932164
  196.9 1.6 copy-start.2
  198.5 25.3 %copy-start.3 = (bf16[64,512]{1,0:T(8,128)(2,1)}, bf16[64,512]{1,0:T(8,128)(2,1)S(1)}, u32[]{:S(2)}) copy-start(bf16[64,512]{1,0:T(8,128)(2,1)S(1)} %get-tuple-element.14) | copy-start | bytes 196612
  199.3 48.8 %copy-start.5 = (bf16[64,512]{1,0:T(8,128)(2,1)}, bf16[64,512]{1,0:T(8,128)(2,1)S(1)}, u32[]{:S(2)}) copy-start(bf16[64,512]{1,0:T(8,128)(2,1)S(1)} %get-tuple-element.15) | copy-start | bytes 196612
  199.4 20.7 %collective-permute-start.19 = (bf16[256,128]{1,0:T(8,128)(2,1)S(1)}, bf16[256,128]{1,0:T(8,128)(2,1)S(1)}, u32[]{:S(2)}, u32[]{:S(2)}) collective-permute-start(bf16[256,128]{1,0:T(8,128)(2,1)S(1)} %get-tuple-element.33), channel_id=1, source_target_pairs={{0,8},{1,9},{2,10},{3,11},{4,12},{5,13},{6,14},{7,15},{8,16},{9,17... | collective-permute-start | bytes 196616 | tf_op jit(solution)/shard_map/ppermute | solution.py:38
  204.8 15.2 %collective-permute-start.20 = (bf16[256,128]{1,0:T(8,128)(2,1)S(1)}, bf16[256,128]{1,0:T(8,128)(2,1)S(1)}, u32[]{:S(2)}, u32[]{:S(2)}) collective-permute-start(bf16[256,128]{1,0:T(8,128)(2,1)S(1)} %get-tuple-element.33), channel_id=1, source_target_pairs={{0,24},{1,25},{2,26},{3,27},{4,28},{5,29},{6,30},{7,31},{8,0},{9,1... | collective-permute-start | bytes 196616 | tf_op jit(solution)/shard_map/ppermute | solution.py:38
  206.8 17.0 %collective-permute-start.21 = (bf16[256,128]{1,0:T(8,128)(2,1)S(1)}, bf16[256,128]{1,0:T(8,128)(2,1)S(1)}, u32[]{:S(2)}, u32[]{:S(2)}) collective-permute-start(bf16[256,128]{1,0:T(8,128)(2,1)S(1)} %get-tuple-element.33), channel_id=1, source_target_pairs={{0,16},{1,17},{2,18},{3,19},{4,20},{5,21},{6,22},{7,23},{8,24},{9,... | collective-permute-start | bytes 196616 | tf_op jit(solution)/shard_map/ppermute | solution.py:38
  224.6 4.2 %collective-permute-start.22 = (bf16[256,256]{1,0:T(8,128)(2,1)S(1)}, bf16[256,256]{1,0:T(8,128)(2,1)S(1)}, u32[]{:S(2)}, u32[]{:S(2)}) collective-permute-start(bf16[256,256]{1,0:T(8,128)(2,1)S(1)} %get-tuple-element.24), channel_id=1, source_target_pairs={{0,64},{1,65},{2,66},{3,67},{4,68},{5,69},{6,70},{7,71},{8,72},{9,... | collective-permute-start | bytes 393224 | tf_op jit(solution)/shard_map/ppermute | solution.py:38
  224.7 7.2 %collective-permute-start.24 = (bf16[256,256]{1,0:T(8,128)(2,1)S(1)}, bf16[256,256]{1,0:T(8,128)(2,1)S(1)}, u32[]{:S(2)}, u32[]{:S(2)}) collective-permute-start(bf16[256,256]{1,0:T(8,128)(2,1)S(1)} %get-tuple-element.25), channel_id=1, source_target_pairs={{0,192},{1,193},{2,194},{3,195},{4,196},{5,197},{6,198},{7,199},{8... | collective-permute-start | bytes 393224 | tf_op jit(solution)/shard_map/ppermute | solution.py:38
  228.8 5.4 %collective-permute-start.23 = (bf16[256,256]{1,0:T(8,128)(2,1)S(1)}, bf16[256,256]{1,0:T(8,128)(2,1)S(1)}, u32[]{:S(2)}, u32[]{:S(2)}) collective-permute-start(bf16[256,256]{1,0:T(8,128)(2,1)S(1)} %add.171), channel_id=1, source_target_pairs={{0,192},{1,193},{2,194},{3,195},{4,196},{5,197},{6,198},{7,199},{8... | collective-permute-start | bytes 393224 | tf_op jit(solution)/shard_map/ppermute | solution.py:38
  232.0 3.9 %collective-permute-start.25 = (bf16[256,256]{1,0:T(8,128)(2,1)S(1)}, bf16[256,256]{1,0:T(8,128)(2,1)S(1)}, u32[]{:S(2)}, u32[]{:S(2)}) collective-permute-start(bf16[256,256]{1,0:T(8,128)(2,1)S(1)} %add.173), channel_id=1, source_target_pairs={{0,64},{1,65},{2,66},{3,67},{4,68},{5,69},{6,70},{7,71},{8,72},{9,... | collective-permute-start | bytes 393224 | tf_op jit(solution)/shard_map/ppermute | solution.py:38
  235.9 14.0 %collective-permute-start.26 = (bf16[2,256,256]{2,1,0:T(8,128)(2,1)S(1)}, bf16[2,256,256]{2,1,0:T(8,128)(2,1)}, u32[]{:S(2)}, u32[]{:S(2)}) collective-permute-start(bf16[2,256,256]{2,1,0:T(8,128)(2,1)S(1)} %pad_maximum_fusion.1.kv), channel_id=1, source_target_pairs={{0,32},{1,33},{2,34},{3,35},{4,36},{5,37},{6,38},{7,39},{8,40},{9,... | collective-permute-start | bytes 786440 | tf_op jit(solution)/shard_map/ppermute | solution.py:38
  248.1 1.8 collective-permute-start.17
  248.1 1.7 copy-start.4
  248.1 1.7 copy-start.6
  249.3 1.6 collective-permute-start.18
  (1 other events, 0.8 us)
